TPU v7x, 32 devices: a whole 2x2x4 slice. The times are simulated.
32 devices in a mesh: dp: 8 (over z, core), tensor: 4 (over y, x).
Axes of the slice: x: 2, y: 2, z: 4, core: 2. Of those that a mesh axis runs over, the one named last changes fastest.
Arguments:
- tokens: bfloat16 [16, 512, 1024], P('dp', 'tensor'), may hold values from -8.5 to 8.5
- segment_ids: int32 [16, 512], P('dp'), may hold values from 0 to 5, never falling along the last dimension, each value on 1 to 128 neighbouring positions
- w_qkv: bfloat16 [3, 1024, 1024], P(None, 'dp', 'tensor'), may hold values from -0.2625 to 0.2625
- w_out: bfloat16 [1024, 1024], P('tensor', 'dp'), may hold values from -1.75 to 1.75
- w_up: bfloat16 [1024, 4096], P('dp', 'tensor'), may hold values from -0.1875 to 0.1875
- w_down: bfloat16 [4096, 1024], P('tensor', 'dp'), may hold values from -0.09375 to 0.09375
- vectors: bfloat16 [12, 1024], P(None, 'dp'), may hold values from -3 to 3
- cotangent: bfloat16 [16, 512, 1024], P('dp', 'tensor'), may hold values from -6 to 6
Outputs:
- out_tokens: bfloat16 [16, 512, 1024], P('dp', 'tensor')
- grad_tokens: float32 [16, 512, 1024], P('dp', 'tensor')
- grad_qkv: float32 [3, 1024, 1024], P(None, 'dp', 'tensor')
- grad_out: float32 [1024, 1024], P('tensor', 'dp')
- grad_up: float32 [1024, 4096], P('dp', 'tensor')
- grad_down: float32 [4096, 1024], P('tensor', 'dp')
- grad_vectors: float32 [12, 1024], P(None, 'dp')
Inputs may be any that keep to these rules, and one draw needn't show every extreme that they name: `segment_ids`: within a sequence the ids never fall; each document has 1 to 128 tokens and one has exactly that many.
All inputs are finite; a program needn't handle non-finite values.
Results may differ from a plain program's by a relative error of at most 0.02.
Values may be sent and summed in bfloat16 or wider, within the bound.
A program may use at most 128 MiB of HBM per device.

v0:
```python
import jax
import jax.numpy as jnp
from jax import lax
from jax.sharding import PartitionSpec as P

D = 1024
FF = 4096
HD = 64


NORM_EPS = 1e-06
SQRT_HALF = 0.7071067811865476
INV_ROOT_TAU = 0.3989422804014327
MASKED = -1e30


def gelu_value(pre_act):
    return 0.5 * pre_act * (1.0 + lax.erf(pre_act * SQRT_HALF))


def gelu_slope(pre_act):
    return 0.5 * (1.0 + lax.erf(pre_act * SQRT_HALF)) + pre_act * INV_ROOT_TAU * jnp.exp(
        -0.5 * pre_act * pre_act
    )


def norm_forward(summed, gain, shift):
    centred = summed - jnp.mean(summed, axis=-1, keepdims=True)
    inverse = lax.rsqrt(jnp.mean(centred * centred, axis=-1, keepdims=True) + NORM_EPS)
    normed = centred * inverse
    return (normed * gain + shift, normed, inverse)


def norm_backward(normed, inverse, grad_normed):
    first_mean = jnp.mean(grad_normed, axis=-1, keepdims=True)
    second_mean = jnp.mean(grad_normed * normed, axis=-1, keepdims=True)
    return inverse * (grad_normed - first_mean - normed * second_mean)


def attention_scores(query_heads, key_heads, segments):
    same_doc = segments[:, None] == segments[None, :]
    scores = jnp.einsum(
        "qhe,khe->hqk", query_heads, key_heads, preferred_element_type=jnp.float32
    ) * HD ** (-0.5)
    return jnp.where(same_doc[None], scores, MASKED)


def collect(w_qkv, w_out, w_up, w_down, vectors):
    return (
        lax.all_gather(w_qkv, "dp", axis=1, tiled=True),
        lax.all_gather(w_out, "dp", axis=1, tiled=True),
        lax.all_gather(w_up, "dp", axis=0, tiled=True),
        lax.all_gather(w_down, "dp", axis=1, tiled=True),
        lax.all_gather(vectors, "dp", axis=1, tiled=True),
    )


def share(gradients):
    return (
        lax.psum_scatter(
            gradients[0].astype(jnp.bfloat16), "dp", scatter_dimension=1, tiled=True
        ).astype(jnp.float32),
        lax.psum_scatter(
            gradients[1].astype(jnp.bfloat16), "dp", scatter_dimension=1, tiled=True
        ).astype(jnp.float32),
        lax.psum_scatter(
            gradients[2].astype(jnp.bfloat16), "dp", scatter_dimension=0, tiled=True
        ).astype(jnp.float32),
        lax.psum_scatter(
            gradients[3].astype(jnp.bfloat16), "dp", scatter_dimension=1, tiled=True
        ).astype(jnp.float32),
        lax.psum_scatter(
            gradients[4].astype(jnp.bfloat16), "dp", scatter_dimension=1, tiled=True
        ).astype(jnp.float32),
    )


def body(tokens, segment_ids, w_qkv, w_out, w_up, w_down, vectors, cotangent):
    tensor_rank = lax.axis_index("tensor")
    local_cols = w_qkv.shape[2]
    head_count = local_cols // HD
    hidden = w_up.shape[1]
    col_start = tensor_rank * local_cols
    ffn_start = tensor_rank * hidden

    def forward(weights, tok_block, segments):
        qkv_w, out_w, up_w, down_w, vec_b = weights
        vec_f32 = vec_b.astype(jnp.float32)
        whole = lax.all_gather(tok_block, "tensor", axis=0, tiled=True)
        seq_len = whole.shape[0]
        projected = jnp.einsum("sd,tdc->tsc", whole, qkv_w, preferred_element_type=jnp.float32)
        bias_q = lax.dynamic_slice_in_dim(vec_f32[0], col_start, local_cols)
        bias_v = lax.dynamic_slice_in_dim(vec_f32[1], col_start, local_cols)
        query_heads = (projected[0] + bias_q).astype(jnp.bfloat16).reshape(seq_len, head_count, HD)
        key_heads = projected[1].astype(jnp.bfloat16).reshape(seq_len, head_count, HD)
        value_heads = (projected[2] + bias_v).astype(jnp.bfloat16).reshape(seq_len, head_count, HD)
        scores = attention_scores(query_heads, key_heads, segments)
        row_top = jnp.max(scores, axis=-1, keepdims=True)
        log_total = row_top + jnp.log(jnp.sum(jnp.exp(scores - row_top), axis=-1, keepdims=True))
        attn_probs = jnp.exp(scores - log_total).astype(jnp.bfloat16)
        context = jnp.einsum(
            "hqk,khe->qhe", attn_probs, value_heads, preferred_element_type=jnp.float32
        )
        context = context.reshape(seq_len, local_cols).astype(jnp.bfloat16)
        piece = context
        attn_mixed = lax.psum_scatter(
            jnp.dot(piece, out_w, preferred_element_type=jnp.float32).astype(jnp.bfloat16),
            "tensor",
            scatter_dimension=0,
            tiled=True,
        ).astype(jnp.float32)
        summed_one = tok_block.astype(jnp.float32) + attn_mixed + vec_f32[2]
        normed_out, normed_one, inverse_one = norm_forward(summed_one, vec_f32[3], vec_f32[4])
        normed_b = normed_out.astype(jnp.bfloat16)
        normed_whole = lax.all_gather(normed_b, "tensor", axis=0, tiled=True)
        bias_up = lax.dynamic_slice_in_dim(vec_f32[8:12].reshape(FF), ffn_start, hidden)
        pre_act = jnp.dot(normed_whole, up_w, preferred_element_type=jnp.float32) + bias_up
        activated = gelu_value(pre_act).astype(jnp.bfloat16)
        piece = activated
        summed_two = (
            normed_out
            + lax.psum_scatter(
                jnp.dot(piece, down_w, preferred_element_type=jnp.float32).astype(jnp.bfloat16),
                "tensor",
                scatter_dimension=0,
                tiled=True,
            ).astype(jnp.float32)
            + vec_f32[5]
        )
        final, normed_two, inverse_two = norm_forward(summed_two, vec_f32[6], vec_f32[7])
        saved = (
            whole,
            query_heads,
            key_heads,
            value_heads,
            log_total,
            context,
            normed_one,
            inverse_one,
            normed_whole,
            pre_act,
            activated,
            normed_two,
            inverse_two,
        )
        return (final.astype(jnp.bfloat16), saved)

    def backward(weights, saved, segments, grad_block):
        qkv_w, out_w, up_w, down_w, vec_b = weights
        vec_f32 = vec_b.astype(jnp.float32)
        (
            whole,
            query_heads,
            key_heads,
            value_heads,
            log_total,
            context,
            normed_one,
            inverse_one,
            normed_whole,
            pre_act,
            activated,
            normed_two,
            inverse_two,
        ) = saved
        seq_len = whole.shape[0]
        grad_final = grad_block.astype(jnp.float32)
        g_gain2 = jnp.sum(grad_final * normed_two, axis=0)
        g_shift2 = jnp.sum(grad_final, axis=0)
        grad_two = norm_backward(normed_two, inverse_two, grad_final * vec_f32[6])
        grad_two_b = grad_two.astype(jnp.bfloat16)
        g_bdown = jnp.sum(grad_two, axis=0)
        grad_two_whole = lax.all_gather(grad_two_b, "tensor", axis=0, tiled=True)
        g_down = jnp.dot(activated.T, grad_two_whole, preferred_element_type=jnp.float32)
        grad_pre = jnp.dot(
            grad_two_whole, down_w.T, preferred_element_type=jnp.float32
        ) * gelu_slope(pre_act)
        grad_pre_b = grad_pre.astype(jnp.bfloat16)
        g_bup = jnp.sum(grad_pre, axis=0)
        g_up = jnp.dot(normed_whole.T, grad_pre_b, preferred_element_type=jnp.float32)
        piece = grad_pre_b
        grad_one_in = grad_two + lax.psum_scatter(
            jnp.dot(piece, up_w.T, preferred_element_type=jnp.float32).astype(jnp.bfloat16),
            "tensor",
            scatter_dimension=0,
            tiled=True,
        ).astype(jnp.float32)
        g_gain1 = jnp.sum(grad_one_in * normed_one, axis=0)
        g_shift1 = jnp.sum(grad_one_in, axis=0)
        grad_one = norm_backward(normed_one, inverse_one, grad_one_in * vec_f32[3])
        grad_one_b = grad_one.astype(jnp.bfloat16)
        g_bout = jnp.sum(grad_one, axis=0)
        grad_one_whole = lax.all_gather(grad_one_b, "tensor", axis=0, tiled=True)
        g_out = jnp.dot(context.T, grad_one_whole, preferred_element_type=jnp.float32)
        grad_context = jnp.dot(grad_one_whole, out_w.T, preferred_element_type=jnp.float32).astype(
            jnp.bfloat16
        )
        grad_context = grad_context.reshape(seq_len, head_count, HD)
        scores = attention_scores(query_heads, key_heads, segments)
        attn_exact = jnp.exp(scores - log_total)
        attn_probs = attn_exact.astype(jnp.bfloat16)
        grad_probs = jnp.einsum(
            "qhe,khe->hqk", grad_context, value_heads, preferred_element_type=jnp.float32
        )
        row_dot = jnp.sum(attn_exact * grad_probs, axis=-1, keepdims=True)
        grad_scores = (attn_exact * (grad_probs - row_dot) * HD ** (-0.5)).astype(jnp.bfloat16)
        grad_value = jnp.einsum(
            "hqk,qhe->khe", attn_probs, grad_context, preferred_element_type=jnp.float32
        )
        grad_value = grad_value.reshape(seq_len, local_cols)
        grad_query = jnp.einsum(
            "hqk,khe->qhe", grad_scores, key_heads, preferred_element_type=jnp.float32
        )
        grad_query = grad_query.reshape(seq_len, local_cols)
        grad_key = jnp.einsum(
            "hqk,qhe->khe", grad_scores, query_heads, preferred_element_type=jnp.float32
        )
        grad_key = grad_key.reshape(seq_len, local_cols)
        grad_qkv = jnp.stack([grad_query, grad_key, grad_value]).astype(jnp.bfloat16)
        g_qkv = jnp.einsum("sd,tsc->tdc", whole, grad_qkv, preferred_element_type=jnp.float32)
        piece = grad_qkv
        grad_input = grad_one + lax.psum_scatter(
            jnp.einsum("tsc,tdc->sd", piece, qkv_w, preferred_element_type=jnp.float32).astype(
                jnp.bfloat16
            ),
            "tensor",
            scatter_dimension=0,
            tiled=True,
        ).astype(jnp.float32)
        zero_row = jnp.zeros((D,), jnp.float32)
        row_q = lax.dynamic_update_slice_in_dim(zero_row, jnp.sum(grad_query, axis=0), col_start, 0)
        row_v = lax.dynamic_update_slice_in_dim(zero_row, jnp.sum(grad_value, axis=0), col_start, 0)
        up_rows = lax.dynamic_update_slice_in_dim(
            jnp.zeros((FF,), jnp.float32), g_bup, ffn_start, 0
        ).reshape(4, D)
        first_rows = jnp.stack(
            [row_q, row_v, g_bout, g_gain1, g_shift1, g_bdown, g_gain2, g_shift2]
        )
        g_vec = jnp.concatenate([first_rows, up_rows], axis=0)
        return ((g_qkv, g_out, g_up, g_down, g_vec), grad_input)

    def one_batch(carried, batch_item):
        tok_block, segments, grad_block = batch_item
        forward_w = collect(w_qkv, w_out, w_up, w_down, vectors)
        final_b, saved = forward(forward_w, tok_block, segments)
        second = collect(w_qkv, w_out, w_up, w_down, vectors)
        gradients, grad_input = backward(second, saved, segments, grad_block)
        updated = jax.tree.map(jnp.add, carried, gradients)
        return (updated, (final_b, grad_input))

    initial = (
        jnp.zeros((3, D, local_cols), jnp.float32),
        jnp.zeros((local_cols, D), jnp.float32),
        jnp.zeros((D, hidden), jnp.float32),
        jnp.zeros((hidden, D), jnp.float32),
        jnp.zeros((12, D), jnp.float32),
    )
    carried, stacked = lax.scan(one_batch, initial, (tokens, segment_ids, cotangent))
    totals = share(carried)
    vector_grads = lax.psum(totals[4], "tensor")
    return (stacked[0], stacked[1], totals[0], totals[1], totals[2], totals[3], vector_grads)


def solution(mesh):
    return jax.shard_map(
        body,
        mesh=mesh,
        in_specs=(
            P("dp", "tensor", None),
            P("dp", None),
            P(None, "dp", "tensor"),
            P("tensor", "dp"),
            P("dp", "tensor"),
            P("tensor", "dp"),
            P(None, "dp"),
            P("dp", "tensor", None),
        ),
        out_specs=(
            P("dp", "tensor", None),
            P("dp", "tensor", None),
            P(None, "dp", "tensor"),
            P("tensor", "dp"),
            P("dp", "tensor"),
            P("tensor", "dp"),
            P(None, "dp"),
        ),
        check_vma=False,
    )
```

profile of v0, /device:TPU:0, one launch (start us, length us, event | category | flops | bytes accessed | tf_op | source)
XLA Modules:
  0.0 942.0 jit_solution(16017847547988003658)
XLA Ops:
  9.8 748.5 %while.25 = (s32[]{:T(128)}, f32[3,1024,256]{1,2,0:T(8,128)}, f32[256,1024]{1,0:T(8,128)}, f32[1024,1024]{1,0:T(8,128)}, f32[1024,1024]{1,0:T(8,128)}, /*index=5...) while((s32[]{:T(128)}, f32[3,1024,256]{1,2,0:T(8,128)}, ...), condition=%wide.region_25.26_spmd.clone, body=%wide.region_0.25_spmd.clone.sunk | while | flops 10544906240 | bytes 269724672 | solution.py:258
  12.3 14.6 %all_gather.66 = bf16[12,1024]{1,0:T(8,128)(2,1)S(1)} all-gather(bf16[12,128]{1,0:T(8,128)(2,1)} %get-tuple-element.627), channel_id=1, replica_groups=mesh['dp'=8,'tensor'=4] {'dp'}, dimensions={1}, use_global_device_ids=true | all-gather | bytes 27648 | tf_op jit(solution)/shard_map/while/body/eval_jaxpr/all_gather | solution.py:54
  27.9 13.9 %all_gather.69 = bf16[256,1024]{1,0:T(8,128)(2,1)S(1)} all-gather(bf16[256,128]{1,0:T(8,128)(2,1)} %get-tuple-element.629), channel_id=1, replica_groups=mesh['dp'=8,'tensor'=4] {'dp'}, dimensions={1}, use_global_device_ids=true | all-gather | bytes 589824 | tf_op jit(solution)/shard_map/while/body/eval_jaxpr/all_gather | solution.py:51
  42.3 28.7 %all-gather.16.cloned.1.call-done = bf16[3,1024,256]{1,2,0:T(8,128)(2,1)} async-done(((bf16[3,128,256]{1,2,0:T(8,128)(2,1)}), bf16[3,1024,256]{1,2,0:T(8,128)(2,1)}) %all-gather.16.cloned.1.call-update) | async-done | bytes 1572880 | tf_op jit(solution)/shard_map/while/body/eval_jaxpr/all_gather | solution.py:50
  79.2 26.3 %reduce-scatter.26.cloned.1.call-done = bf16[128,1024]{1,0:T(8,128)(2,1)} async-done(((bf16[512,1024]{1,0:T(8,128)(2,1)}), bf16[128,1024]{1,0:T(8,128)(2,1)}) %reduce-scatter.26.cloned.1.call-update) | async-done | bytes 262160 | tf_op jit(solution)/shard_map/while/body/eval_jaxpr/reduce_scatter | solution.py:106
  110.3 25.8 %all-gather.20.cloned.1.call-done = bf16[1024,1024]{1,0:T(8,128)(2,1)} async-done(((bf16[128,1024]{1,0:T(8,128)(2,1)}), bf16[1024,1024]{1,0:T(8,128)(2,1)}) %all-gather.20.cloned.1.call-update) | async-done | bytes 2097168 | tf_op jit(solution)/shard_map/while/body/eval_jaxpr/all_gather | solution.py:52
  136.2 28.2 %all-gather.18.cloned.1.call-done = bf16[512,1024]{1,0:T(8,128)(2,1)} async-done(((bf16[128,1024]{1,0:T(8,128)(2,1)}), bf16[512,1024]{1,0:T(8,128)(2,1)}) %all-gather.18.cloned.1.call-update) | async-done | bytes 1048592 | tf_op jit(solution)/shard_map/while/body/eval_jaxpr/all_gather | solution.py:115
  168.9 27.5 %all-gather.14.cloned.1.call-done = bf16[1024,1024]{1,0:T(8,128)(2,1)} async-done(((bf16[1024,128]{1,0:T(8,128)(2,1)}), bf16[1024,1024]{1,0:T(8,128)(2,1)}) %all-gather.14.cloned.1.call-update) | async-done | bytes 2097168 | tf_op jit(solution)/shard_map/while/body/eval_jaxpr/all_gather | solution.py:53
  201.0 27.1 %reduce-scatter.28.cloned.1.call-done = bf16[128,1024]{1,0:T(8,128)(2,1)} async-done(((bf16[512,1024]{1,0:T(8,128)(2,1)}), bf16[128,1024]{1,0:T(8,128)(2,1)}) %reduce-scatter.28.cloned.1.call-update) | async-done | bytes 262160 | tf_op jit(solution)/shard_map/while/body/eval_jaxpr/reduce_scatter | solution.py:122
  232.4 26.6 %all-gather.22.cloned.1.call-done = bf16[512,1024]{1,0:T(8,128)(2,1)} async-done(((bf16[128,1024]{1,0:T(8,128)(2,1)}), bf16[512,1024]{1,0:T(8,128)(2,1)}) %all-gather.22.cloned.1.call-update) | async-done | bytes 1048592 | tf_op jit(solution)/shard_map/while/body/eval_jaxpr/all_gather | solution.py:173
  266.9 28.0 %reduce-scatter.30.cloned.1.call-done = bf16[128,1024]{1,0:T(8,128)(2,1)} async-done(((bf16[512,1024]{1,0:T(8,128)(2,1)}), bf16[128,1024]{1,0:T(8,128)(2,1)}) %reduce-scatter.30.cloned.1.call-update) | async-done | bytes 262160 | tf_op jit(solution)/shard_map/while/body/eval_jaxpr/reduce_scatter | solution.py:182
  303.1 23.9 %all-gather.24.cloned.1.call-done = bf16[512,1024]{1,0:T(8,128)(2,1)} async-done(((bf16[128,1024]{1,0:T(8,128)(2,1)}), bf16[512,1024]{1,0:T(8,128)(2,1)}) %all-gather.24.cloned.1.call-update) | async-done | bytes 1048592 | tf_op jit(solution)/shard_map/while/body/eval_jaxpr/all_gather | solution.py:193
  343.1 8.8 fusion.174
  370.7 12.9 %reduce-scatter.32.cloned.1.call-done = bf16[128,1024]{1,0:T(8,128)(2,1)} async-done(((bf16[512,1024]{1,0:T(8,128)(2,1)}), bf16[128,1024]{1,0:T(8,128)(2,1)}) %reduce-scatter.32.cloned.1.call-update) | async-done | bytes 262160 | tf_op jit(solution)/shard_map/while/body/eval_jaxpr/reduce_scatter | solution.py:222
  388.1 13.0 %all_gather.66 = bf16[12,1024]{1,0:T(8,128)(2,1)S(1)} all-gather(bf16[12,128]{1,0:T(8,128)(2,1)} %get-tuple-element.627), channel_id=1, replica_groups=mesh['dp'=8,'tensor'=4] {'dp'}, dimensions={1}, use_global_device_ids=true | all-gather | bytes 27648 | tf_op jit(solution)/shard_map/while/body/eval_jaxpr/all_gather | solution.py:54
  402.0 14.0 %all_gather.69 = bf16[256,1024]{1,0:T(8,128)(2,1)S(1)} all-gather(bf16[256,128]{1,0:T(8,128)(2,1)} %get-tuple-element.629), channel_id=1, replica_groups=mesh['dp'=8,'tensor'=4] {'dp'}, dimensions={1}, use_global_device_ids=true | all-gather | bytes 589824 | tf_op jit(solution)/shard_map/while/body/eval_jaxpr/all_gather | solution.py:51
  416.2 27.5 %all-gather.16.cloned.1.call-done = bf16[3,1024,256]{1,2,0:T(8,128)(2,1)} async-done(((bf16[3,128,256]{1,2,0:T(8,128)(2,1)}), bf16[3,1024,256]{1,2,0:T(8,128)(2,1)}) %all-gather.16.cloned.1.call-update) | async-done | bytes 1572880 | tf_op jit(solution)/shard_map/while/body/eval_jaxpr/all_gather | solution.py:50
  452.0 26.3 %reduce-scatter.26.cloned.1.call-done = bf16[128,1024]{1,0:T(8,128)(2,1)} async-done(((bf16[512,1024]{1,0:T(8,128)(2,1)}), bf16[128,1024]{1,0:T(8,128)(2,1)}) %reduce-scatter.26.cloned.1.call-update) | async-done | bytes 262160 | tf_op jit(solution)/shard_map/while/body/eval_jaxpr/reduce_scatter | solution.py:106
  483.1 25.8 %all-gather.20.cloned.1.call-done = bf16[1024,1024]{1,0:T(8,128)(2,1)} async-done(((bf16[128,1024]{1,0:T(8,128)(2,1)}), bf16[1024,1024]{1,0:T(8,128)(2,1)}) %all-gather.20.cloned.1.call-update) | async-done | bytes 2097168 | tf_op jit(solution)/shard_map/while/body/eval_jaxpr/all_gather | solution.py:52
  508.9 28.2 %all-gather.18.cloned.1.call-done = bf16[512,1024]{1,0:T(8,128)(2,1)} async-done(((bf16[128,1024]{1,0:T(8,128)(2,1)}), bf16[512,1024]{1,0:T(8,128)(2,1)}) %all-gather.18.cloned.1.call-update) | async-done | bytes 1048592 | tf_op jit(solution)/shard_map/while/body/eval_jaxpr/all_gather | solution.py:115
  541.6 27.5 %all-gather.14.cloned.1.call-done = bf16[1024,1024]{1,0:T(8,128)(2,1)} async-done(((bf16[1024,128]{1,0:T(8,128)(2,1)}), bf16[1024,1024]{1,0:T(8,128)(2,1)}) %all-gather.14.cloned.1.call-update) | async-done | bytes 2097168 | tf_op jit(solution)/shard_map/while/body/eval_jaxpr/all_gather | solution.py:53
  573.7 27.1 %reduce-scatter.28.cloned.1.call-done = bf16[128,1024]{1,0:T(8,128)(2,1)} async-done(((bf16[512,1024]{1,0:T(8,128)(2,1)}), bf16[128,1024]{1,0:T(8,128)(2,1)}) %reduce-scatter.28.cloned.1.call-update) | async-done | bytes 262160 | tf_op jit(solution)/shard_map/while/body/eval_jaxpr/reduce_scatter | solution.py:122
  605.0 26.6 %all-gather.22.cloned.1.call-done = bf16[512,1024]{1,0:T(8,128)(2,1)} async-done(((bf16[128,1024]{1,0:T(8,128)(2,1)}), bf16[512,1024]{1,0:T(8,128)(2,1)}) %all-gather.22.cloned.1.call-update) | async-done | bytes 1048592 | tf_op jit(solution)/shard_map/while/body/eval_jaxpr/all_gather | solution.py:173
  639.6 28.0 %reduce-scatter.30.cloned.1.call-done = bf16[128,1024]{1,0:T(8,128)(2,1)} async-done(((bf16[512,1024]{1,0:T(8,128)(2,1)}), bf16[128,1024]{1,0:T(8,128)(2,1)}) %reduce-scatter.30.cloned.1.call-update) | async-done | bytes 262160 | tf_op jit(solution)/shard_map/while/body/eval_jaxpr/reduce_scatter | solution.py:182
  675.8 23.9 %all-gather.24.cloned.1.call-done = bf16[512,1024]{1,0:T(8,128)(2,1)} async-done(((bf16[128,1024]{1,0:T(8,128)(2,1)}), bf16[512,1024]{1,0:T(8,128)(2,1)}) %all-gather.24.cloned.1.call-update) | async-done | bytes 1048592 | tf_op jit(solution)/shard_map/while/body/eval_jaxpr/all_gather | solution.py:193
  715.8 8.8 fusion.174
  774.5 17.9 %reduce-scatter.24.cloned.1.call-done = bf16[128,12]{1,0:T(8,128)(2,1)} async-done(((bf16[1024,12]{1,0:T(8,128)(2,1)}), bf16[128,12]{1,0:T(8,128)(2,1)}) %reduce-scatter.24.cloned.1.call-update) | async-done | bytes 3088
  793.2 10.6 %psum.7 = f32[12,128]{1,0:T(8,128)} all-reduce(bf16[12,128]{1,0:T(8,128)(2,1)S(1)} %copy.42), channel_id=1, replica_groups=mesh['dp'=8,'tensor'=4] {'tensor'}, use_global_device_ids=true, to_apply=%region_31.32 | all-reduce | flops 1536 | bytes 9216 | tf_op jit(solution)/shard_map/psum | solution.py:260
  803.8 20.7 %reduce-scatter.20.cloned.1.call-done = bf16[128,256]{1,0:T(8,128)(2,1)} async-done(((bf16[1024,256]{1,0:T(8,128)(2,1)}), bf16[128,256]{1,0:T(8,128)(2,1)}) %reduce-scatter.20.cloned.1.call-update) | async-done | bytes 65552
  826.1 32.9 %reduce-scatter.16.cloned.1.call-done = bf16[3,128,256]{2,1,0:T(8,128)(2,1)} async-done(((bf16[3,1024,256]{2,1,0:T(8,128)(2,1)}), bf16[3,128,256]{2,1,0:T(8,128)(2,1)}) %reduce-scatter.16.cloned.1.call-update) | async-done | bytes 196624 | tf_op jit(solution)/shard_map/reduce_scatter | solution.py:60
  860.7 35.1 %reduce-scatter.22.cloned.1.call-done = bf16[128,1024]{1,0:T(8,128)(2,1)} async-done(((bf16[1024,1024]{1,0:T(8,128)(2,1)}), bf16[128,1024]{1,0:T(8,128)(2,1)}) %reduce-scatter.22.cloned.1.call-update) | async-done | bytes 262160
  897.7 34.9 %reduce-scatter.18.cloned.1.call-done = bf16[128,1024]{1,0:T(8,128)(2,1)} async-done(((bf16[1024,1024]{1,0:T(8,128)(2,1)}), bf16[128,1024]{1,0:T(8,128)(2,1)}) %reduce-scatter.18.cloned.1.call-update) | async-done | bytes 262160 | tf_op jit(solution)/shard_map/reduce_scatter | solution.py:66
  (318 shorter events, 204.2 us)
Async XLA Ops:
  9.8 32.5 %all-gather.12.cloned.1.call-start = ((), (), s32[]{:S(2)}) async-start(), calls=%async_computation.14 | async-start | bytes 1310720 | tf_op jit(solution)/shard_map/while/body/eval_jaxpr/all_gather | solution.py:89
  11.5 59.5 %all-gather.16.cloned.1.call-start = ((), (), s32[]{:S(2)}) async-start(), calls=%async_computation.16 | async-start | bytes 1769472 | tf_op jit(solution)/shard_map/while/body/eval_jaxpr/all_gather | solution.py:50
  12.3 93.2 %reduce-scatter.26.cloned.1.call-start = ((), (), s32[]{:S(2)}) async-start(), calls=%async_computation.17 | async-start | bytes 1310720 | tf_op jit(solution)/shard_map/while/body/eval_jaxpr/reduce_scatter | solution.py:106
  78.6 57.6 %all-gather.20.cloned.1.call-start = ((), (), s32[]{:S(2)}) async-start(), calls=%async_computation.19 | async-start | bytes 2359296 | tf_op jit(solution)/shard_map/while/body/eval_jaxpr/all_gather | solution.py:52
  79.2 85.2 %all-gather.18.cloned.1.call-start = ((), (), s32[]{:S(2)}) async-start(), calls=%async_computation.18 | async-start | bytes 1310720 | tf_op jit(solution)/shard_map/while/body/eval_jaxpr/all_gather | solution.py:115
  109.7 86.8 %all-gather.14.cloned.1.call-start = ((), (), s32[]{:S(2)}) async-start(), calls=%async_computation.15 | async-start | bytes 2359296 | tf_op jit(solution)/shard_map/while/body/eval_jaxpr/all_gather | solution.py:53
  110.2 117.9 %reduce-scatter.28.cloned.1.call-start = ((), (), s32[]{:S(2)}) async-start(), calls=%async_computation.20 | async-start | bytes 1310720 | tf_op jit(solution)/shard_map/while/body/eval_jaxpr/reduce_scatter | solution.py:122
  168.9 59.2 %copy-start.1 = (bf16[128,1024]{1,0:T(8,128)(2,1)S(1)}, bf16[128,1024]{1,0:T(8,128)(2,1)}, u32[]{:S(2)}) copy-start(bf16[128,1024]{1,0:T(8,128)(2,1)} %reduce-scatter.26.cloned.1.call-done) | copy-start | bytes 786436 | tf_op jit(solution)/shard_map/while
  168.9 60.7 %copy-start.11 = (bf16[2,128,1024]{2,1,0:T(8,128)(2,1)S(1)}, bf16[2,128,1024]{2,1,0:T(8,128)(2,1)}, u32[]{:S(2)}) copy-start(bf16[2,128,1024]{2,1,0:T(8,128)(2,1)} %get-tuple-element.633) | copy-start | bytes 1572868 | tf_op jit(solution)/shard_map/while
  201.0 58.0 %all-gather.22.cloned.1.call-start = ((), (), s32[]{:S(2)}) async-start(), calls=%async_computation.21 | async-start | bytes 1310720 | tf_op jit(solution)/shard_map/while/body/eval_jaxpr/all_gather | solution.py:173
  232.3 62.6 %reduce-scatter.30.cloned.1.call-start = ((), (), s32[]{:S(2)}) async-start(), calls=%async_computation.22 | async-start | bytes 1310720 | tf_op jit(solution)/shard_map/while/body/eval_jaxpr/reduce_scatter | solution.py:182
  266.9 61.8 %copy-start.26 = (f32[4,512]{1,0:T(4,128)S(1)}, f32[4,512]{1,0:T(4,128)}, u32[]{:S(2)}) copy-start(f32[4,512]{1,0:T(4,128)} %copy-done.25) | copy-start | bytes 24580 | tf_op jit(solution)/shard_map/while
  266.9 60.0 %all-gather.24.cloned.1.call-start = ((), (), s32[]{:S(2)}) async-start(), calls=%async_computation.23 | async-start | bytes 1310720 | tf_op jit(solution)/shard_map/while/body/eval_jaxpr/all_gather | solution.py:193
  300.3 83.3 %reduce-scatter.32.cloned.1.call-start = ((), (), s32[]{:S(2)}) async-start(), calls=%async_computation.24 | async-start | bytes 1310720 | tf_op jit(solution)/shard_map/while/body/eval_jaxpr/reduce_scatter | solution.py:222
  385.6 30.6 %all-gather.12.cloned.1.call-start = ((), (), s32[]{:S(2)}) async-start(), calls=%async_computation.14 | async-start | bytes 1310720 | tf_op jit(solution)/shard_map/while/body/eval_jaxpr/all_gather | solution.py:89
  387.3 56.4 %all-gather.16.cloned.1.call-start = ((), (), s32[]{:S(2)}) async-start(), calls=%async_computation.16 | async-start | bytes 1769472 | tf_op jit(solution)/shard_map/while/body/eval_jaxpr/all_gather | solution.py:50
  388.0 90.2 %reduce-scatter.26.cloned.1.call-start = ((), (), s32[]{:S(2)}) async-start(), calls=%async_computation.17 | async-start | bytes 1310720 | tf_op jit(solution)/shard_map/while/body/eval_jaxpr/reduce_scatter | solution.py:106
  451.3 57.5 %all-gather.20.cloned.1.call-start = ((), (), s32[]{:S(2)}) async-start(), calls=%async_computation.19 | async-start | bytes 2359296 | tf_op jit(solution)/shard_map/while/body/eval_jaxpr/all_gather | solution.py:52
  451.9 85.1 %all-gather.18.cloned.1.call-start = ((), (), s32[]{:S(2)}) async-start(), calls=%async_computation.18 | async-start | bytes 1310720 | tf_op jit(solution)/shard_map/while/body/eval_jaxpr/all_gather | solution.py:115
  482.4 86.8 %all-gather.14.cloned.1.call-start = ((), (), s32[]{:S(2)}) async-start(), calls=%async_computation.15 | async-start | bytes 2359296 | tf_op jit(solution)/shard_map/while/body/eval_jaxpr/all_gather | solution.py:53
  483.0 117.8 %reduce-scatter.28.cloned.1.call-start = ((), (), s32[]{:S(2)}) async-start(), calls=%async_computation.20 | async-start | bytes 1310720 | tf_op jit(solution)/shard_map/while/body/eval_jaxpr/reduce_scatter | solution.py:122
  541.6 60.7 %copy-start.11 = (bf16[2,128,1024]{2,1,0:T(8,128)(2,1)S(1)}, bf16[2,128,1024]{2,1,0:T(8,128)(2,1)}, u32[]{:S(2)}) copy-start(bf16[2,128,1024]{2,1,0:T(8,128)(2,1)} %get-tuple-element.633) | copy-start | bytes 1572868 | tf_op jit(solution)/shard_map/while
  573.7 58.0 %all-gather.22.cloned.1.call-start = ((), (), s32[]{:S(2)}) async-start(), calls=%async_computation.21 | async-start | bytes 1310720 | tf_op jit(solution)/shard_map/while/body/eval_jaxpr/all_gather | solution.py:173
  605.0 62.6 %reduce-scatter.30.cloned.1.call-start = ((), (), s32[]{:S(2)}) async-start(), calls=%async_computation.22 | async-start | bytes 1310720 | tf_op jit(solution)/shard_map/while/body/eval_jaxpr/reduce_scatter | solution.py:182
  639.5 61.8 %copy-start.26 = (f32[4,512]{1,0:T(4,128)S(1)}, f32[4,512]{1,0:T(4,128)}, u32[]{:S(2)}) copy-start(f32[4,512]{1,0:T(4,128)} %copy-done.25) | copy-start | bytes 24580 | tf_op jit(solution)/shard_map/while
  639.6 60.0 %all-gather.24.cloned.1.call-start = ((), (), s32[]{:S(2)}) async-start(), calls=%async_computation.23 | async-start | bytes 1310720 | tf_op jit(solution)/shard_map/while/body/eval_jaxpr/all_gather | solution.py:193
  673.0 83.4 %reduce-scatter.32.cloned.1.call-start = ((), (), s32[]{:S(2)}) async-start(), calls=%async_computation.24 | async-start | bytes 1310720 | tf_op jit(solution)/shard_map/while/body/eval_jaxpr/reduce_scatter | solution.py:222
  758.3 34.0 %reduce-scatter.24.cloned.1.call-start = ((), (), s32[]{:S(2)}) async-start(), calls=%async_computation.13 | async-start | bytes 294912
  759.3 65.2 %reduce-scatter.20.cloned.1.call-start = ((), (), s32[]{:S(2)}) async-start(), calls=%async_computation.11 | async-start | bytes 589824
  763.5 95.5 %reduce-scatter.16.cloned.1.call-start = ((), (), s32[]{:S(2)}) async-start(), calls=%async_computation.9 | async-start | bytes 1769472 | tf_op jit(solution)/shard_map/reduce_scatter | solution.py:60
  765.3 130.5 %reduce-scatter.22.cloned.1.call-start = ((), (), s32[]{:S(2)}) async-start(), calls=%async_computation.12 | async-start | bytes 2359296
  770.5 162.1 %reduce-scatter.18.cloned.1.call-start = ((), (), s32[]{:S(2)}) async-start(), calls=%async_computation.10 | async-start | bytes 2359296 | tf_op jit(solution)/shard_map/reduce_scatter | solution.py:66
  (50 other events, 625.2 us)
Sparse Core Ops, SparseCore 0:
  13.0 29.2 all-gather.11
  43.9 27.0 all-gather.15
  78.7 26.7 reduce-scatter.25
  107.0 29.1 all-gather.19
  138.4 25.8 all-gather.17
  165.8 30.5 all-gather.13
  201.1 26.9 reduce-scatter.27
  232.4 26.4 all-gather.21
  267.0 27.9 reduce-scatter.29
  300.4 26.4 all-gather.23
  355.6 27.9 reduce-scatter.31
  388.5 26.4 all-gather.11
  416.6 27.0 all-gather.15
  451.4 26.7 reduce-scatter.25
  479.7 29.1 all-gather.19
  511.1 25.8 all-gather.17
  538.5 30.5 all-gather.13
  573.8 26.9 reduce-scatter.27
  605.1 26.4 all-gather.21
  639.7 27.9 reduce-scatter.29
  673.1 26.4 all-gather.23
  728.3 27.9 reduce-scatter.31
Sparse Core Ops, SparseCore 1:
  761.6 30.7 reduce-scatter.23
  795.1 29.4 reduce-scatter.19
  826.7 32.3 reduce-scatter.15
  861.3 34.4 reduce-scatter.21
  898.1 34.4 reduce-scatter.17
where the time goes:
time: 944 us; the launch traced here: 942 us
  waiting for transfers between devices  649 us (69%)
  matrix products  131 us (14%)
  blocking collectives  66.2 us (7%)
  other arithmetic  50.2 us (5%)
  local copies, waits for them, and re-layouts  27.1 us (3%)
  between operations  15.8 us (2%)
    unnamed x8, waiting for transfers between devices  73.8 us
    all_gather x2, waiting for transfers between devices, forward(): normed_whole = lax.all_gather(normed_b, 'tensor', axis=0, tiled=True)  56.4 us
    all_gather x2, waiting for transfers between devices, collect(): lax.all_gather(w_qkv, 'dp', axis=1, tiled=True)  56.2 us
    reduce_scatter x2, waiting for transfers between devices, backward(): lax.psum_scatter(jnp.dot(piece, up_w.T, preferred_element_type=jnp.float3...  56.1 us
    all_gather x2, waiting for transfers between devices, collect(): lax.all_gather(w_down, 'dp', axis=1, tiled=True)  55.1 us
    reduce_scatter x2, waiting for transfers between devices, forward(): lax.psum_scatter(jnp.dot(piece, down_w, preferred_element_type=jnp.float3...  54.1 us
    all_gather x2, waiting for transfers between devices, backward(): grad_two_whole = lax.all_gather(grad_two_b, 'tensor', axis=0, tiled=True)  53.2 us
    reduce_scatter x2, waiting for transfers between devices, forward(): lax.psum_scatter(jnp.dot(piece, out_w, preferred_element_type=jnp.float32...  52.5 us
  transfers between devices with their start and end apart: 27, of which 26 were waited for; matrix products, arithmetic and copies ran while one was open for 8% of the time, Pallas kernels for 0%

commit v1 on v0

--- a/solution.py
+++ b/solution.py
@@ -1,6 +1,8 @@
 import jax
 import jax.numpy as jnp
 from jax import lax
+from jax.experimental import pallas as pl
+from jax.experimental.pallas import tpu as pltpu
 from jax.sharding import PartitionSpec as P
 
 D = 1024
@@ -261,9 +263,712 @@
     return (stacked[0], stacked[1], totals[0], totals[1], totals[2], totals[3], vector_grads)
 
 
+Y_TOK, Y_COT, Y_OUT, Y_GTOK = range(4)
+X_TOK, X_MIX, X_NORM, X_FFN, X_DA2, X_DH, X_DA1, X_DX = range(8)
+QKV, OUT, UP, DOWN, VEC = range(5)
+U_DOWN, U_UP, U_OUT, U_V, U_K, U_Q = range(6)
+R_BQ, R_BV, R_BO, R_G1, R_C1, R_BD, R_G2, R_C2, R_BU = range(9)
+ZS = 4
+SEQ = 512
+ROWS = 256
+CHUNK = 128
+TILE = 32
+COLS = 512
+HID = 2048
+WINDOW = 384
+BF = jnp.bfloat16
+F32 = jnp.float32
+MESH = pl.DeviceIdType.MESH
+
+
+def span(index, size):
+    return pl.ds(pl.multiple_of(index * size, size), size)
+
+
+def contract(a, b, a_dim, b_dim):
+    return lax.dot_general(a, b, (((a_dim,), (b_dim,)), ((), ())), preferred_element_type=F32)
+
+
+def fold_rows(value):
+    return jnp.sum(value.reshape(value.shape[0] // 8, 8, value.shape[1]), axis=0)
+
+
+def layer_kernel(
+    tok, seg, wq, wo, wu, wd, vec, cot,
+    out, gtok, gq, go, gu, gd, gv,
+    w_qkv, w_out, w_up, w_down, w_vec, vf,
+    g_down, g_up, g_out, g_qkv,
+    c_down, c_up, c_out, c_qkv,
+    y_down, y_up, y_out, y_qkv,
+    z_down, z_up, z_out, z_qkv,
+    o_qkv, o_out, o_up, o_down,
+    xw, qkv, ctx, prob, bias, hw, act, slope, aw, a1w, dctx,
+    own, n1, da, inv1, recv, stage, cotb, outb, gts, gtr, gtf,
+    acc, vg, vgx, vgc, vgy, vgz, gvb, acc_k, acc_v,
+    wsz, wrz, wsy, wry, wsc, wrc, xs, xr, ys, yr,
+    gsc, grc, gsy, gry, gsz, grz, vs, vr, ls, os,
+):
+    dp = lax.axis_index("dp")
+    tensor = lax.axis_index("tensor")
+    z, c = dp // 2, dp % 2
+    y, x = tensor // 2, tensor % 2
+    at_x = {"dp": dp, "tensor": y * 2 + (1 - x)}
+    at_y = {"dp": dp, "tensor": (1 - y) * 2 + x}
+    at_c = {"dp": z * 2 + (1 - c), "tensor": tensor}
+    at_z = [{"dp": lax.rem(z + k, ZS) * 2 + c, "tensor": tensor} for k in range(1, ZS)]
+
+    def remote(src, dst, send, recv_sem, where):
+        return pltpu.make_async_remote_copy(
+            src_ref=src, dst_ref=dst, send_sem=send, recv_sem=recv_sem,
+            device_id=where, device_id_type=MESH,
+        )
+
+    barrier = pltpu.get_barrier_semaphore()
+    for where in [at_x, at_y, at_c] + at_z:
+        pl.semaphore_signal(barrier, inc=1, device_id=where, device_id_type=MESH)
+    pl.semaphore_wait(barrier, 6)
+
+    sent = []
+
+    def go_on(copy):
+        copy.start()
+        sent.append(copy)
+
+    args = [wq, wo, wu, wd, vec]
+
+    def place(m, yy, d):
+        if m == QKV:
+            return w_qkv.at[:, span(d, 128), span(yy, 256)]
+        if m == OUT:
+            return w_out.at[span(yy, 256), span(d, 128)]
+        if m == UP:
+            return w_up.at[span(d, 128), span(yy, 1024)]
+        if m == DOWN:
+            return w_down.at[span(yy, 1024), span(d, 128)]
+        return w_vec.at[d]
+
+    def from_z(k):
+        return lax.rem(z + ZS - k, ZS)
+
+    def z_copy(m, k):
+        return remote(args[m], place(m, y, dp), wsz.at[m, k - 1], wrz.at[m, k - 1], at_z[k - 1])
+
+    def z_arrived(m, k):
+        here = place(m, y, from_z(k) * 2 + c)
+        remote(args[m], here, wsz.at[m, k - 1], wrz.at[m, k - 1], at_z[k - 1]).wait_recv()
+
+    def y_copy(m, j):
+        if j == 0:
+            return remote(args[m], place(m, y, dp), wsy.at[m, 0], wry.at[m, 0], at_y)
+        here = place(m, y, from_z(j) * 2 + c)
+        return remote(here, here, wsy.at[m, j], wry.at[m, j], at_y)
+
+    def y_place(m, j):
+        return place(m, 1 - y, (z if j == 0 else from_z(j)) * 2 + c)
+
+    def y_arrived(m, j):
+        here = y_place(m, j)
+        remote(here, here, wsy.at[m, j], wry.at[m, j], at_y).wait_recv()
+
+    def c_copy(m, j):
+        if j == 0:
+            return remote(args[m], place(m, y, dp), wsc.at[m, 0], wrc.at[m, 0], at_c)
+        here = place(m, y, from_z(j) * 2 + c) if j < 4 else y_place(m, j - 4)
+        return remote(here, here, wsc.at[m, j], wrc.at[m, j], at_c)
+
+    def c_arrived(m, j):
+        d = (z if j == 0 or j == 4 else from_z(j % 4)) * 2 + 1 - c
+        here = place(m, y if j < 4 else 1 - y, d)
+        remote(here, here, wsc.at[m, j], wrc.at[m, j], at_c).wait_recv()
+
+    def serve_z(m, ks=(1, 2, 3)):
+        for k in ks:
+            z_arrived(m, k)
+            if m != VEC:
+                go_on(y_copy(m, k))
+            go_on(c_copy(m, k))
+
+    def serve_y(m):
+        for j in range(4):
+            y_arrived(m, j)
+            go_on(c_copy(m, j + 4))
+
+    def wait_weight(m):
+        if m != VEC:
+            pltpu.make_async_copy(args[m], place(m, y, dp), ls.at[m]).wait()
+        else:
+            pltpu.make_async_copy(args[m], place(m, y, dp), ls.at[m]).wait()
+        for j in range(4 if m == VEC else 8):
+            c_arrived(m, j)
+
+    def x_copy(kind, j, src, dst):
+        return remote(src, dst, xs.at[kind, j], xr.at[kind, j], at_x)
+
+    def tok_rows(xx, yy):
+        return pl.ds(pl.multiple_of(xx * ROWS + yy * CHUNK, CHUNK), CHUNK)
+
+    y_tok = remote(tok.at[1 - y], xw.at[tok_rows(x, y)], ys.at[Y_TOK], yr.at[Y_TOK], at_y)
+    go_on(y_tok)
+    go_on(x_copy(X_TOK, 0, tok.at[y], xw.at[tok_rows(x, y)]))
+    local_x = pltpu.make_async_copy(tok.at[y], xw.at[tok_rows(x, y)], ls.at[5])
+    local_x.start()
+    for m in (QKV, VEC, OUT, UP, DOWN):
+        for k in range(1, ZS):
+            go_on(z_copy(m, k))
+        if m == QKV:
+            go_on(y_copy(m, 0))
+        go_on(c_copy(m, 0))
+        pltpu.make_async_copy(args[m], place(m, y, dp), ls.at[m]).start()
+    local_cot = pltpu.make_async_copy(cot.at[y], cotb.at[span(y, CHUNK)], ls.at[6])
+    local_cot.start()
+
+    seg_row = seg[pl.ds(y, 1), :].astype(F32)
+    blocks = [(p % 2) * 2 + p // 2 for p in range(4)]
+    across = [jnp.broadcast_to(seg_row[:, n * 128:(n + 1) * 128], (128, 128)) for n in blocks]
+    down = [b.T for b in across]
+    for t in range(2):
+        for i, q in enumerate((t, t + 2)):
+            for j in range(3):
+                same = down[q] == across[t + j]
+                bias[t, i * 128:(i + 1) * 128, j * 128:(j + 1) * 128] = jnp.where(same, 0.0, MASKED)
+    acc[...] = jnp.zeros_like(acc)
+    vg[...] = jnp.zeros_like(vg)
+
+    y_tok_here = xw.at[tok_rows(x, 1 - y)]
+    remote(tok.at[1 - y], y_tok_here, ys.at[Y_TOK], yr.at[Y_TOK], at_y).wait_recv()
+    go_on(x_copy(X_TOK, 1, y_tok_here, y_tok_here))
+    serve_z(QKV)
+    serve_z(VEC)
+    go_on(y_copy(OUT, 0))
+    serve_z(OUT)
+    go_on(y_copy(UP, 0))
+    serve_y(QKV)
+    wait_weight(VEC)
+    for d in range(8):
+        vf[0:12, d * 128:(d + 1) * 128] = w_vec[d].astype(F32)
+    local_x.wait()
+    for j, yy in ((0, y), (1, 1 - y)):
+        there = xw.at[tok_rows(1 - x, yy)]
+        x_copy(X_TOK, j, there, there).wait_recv()
+    wait_weight(QKV)
+
+    zero_bias = jnp.zeros((1, COLS), F32)
+
+    def head_bias(row):
+        parts = [vf[row:row + 1, pl.ds(pl.multiple_of(yy * 512 + x * 256, 256), 256)] for yy in range(2)]
+        return jnp.concatenate(parts, axis=1)
+
+    for i in range(3):
+        value = contract(xw[...], w_qkv[i], 1, 0)
+        if i == 0:
+            value = (value + head_bias(0)).astype(BF) * BF(HD ** -0.5)
+        elif i == 2:
+            value = value + head_bias(1)
+        qkv[i] = value.astype(BF)
+
+    low_half = lax.broadcasted_iota(jnp.int32, (1, 128), 1) < HD
+    halves = (low_half, jnp.logical_not(low_half))
+    none = jnp.zeros((), BF)
+
+    def two_blocks(ref, t, lanes):
+        return jnp.concatenate([ref[span(t, 128), lanes], ref[span(t + 2, 128), lanes]], axis=0)
+
+    def attend(index, carry):
+        pair, t = index // 2, index % 2
+        lanes = span(pair, 128)
+        keys = pl.ds(pl.multiple_of(t * 128, 128), WINDOW)
+        query = two_blocks(qkv.at[0], t, lanes)
+        key, value = qkv[1, keys, lanes], qkv[2, keys, lanes]
+        total = jnp.zeros((ROWS, 128), F32)
+        for h, half in enumerate(halves):
+            scores = contract(jnp.where(half, query, none), key, 1, 1) + bias[t]
+            top = jnp.max(scores, axis=1, keepdims=True)
+            weight = jnp.exp(scores - top)
+            share_of = 1.0 / jnp.sum(weight, axis=1, keepdims=True)
+            weight = (weight * share_of).astype(BF)
+            prob[pair * 4 + t * 2 + h] = weight
+            total = total + contract(weight, jnp.where(half, value, none), 1, 0)
+        total = total.astype(BF)
+        ctx[span(t, 128), lanes] = total[:128]
+        ctx[span(t + 2, 128), lanes] = total[128:]
+        return carry
+
+    lax.fori_loop(0, 8, attend, 0)
+
+    def rows_of(s):
+        mine = jnp.where(s < 2, x, 1 - x)
+        return pl.ds(pl.multiple_of(mine * ROWS + lax.rem(s, 2) * CHUNK, CHUNK), CHUNK)
+
+    def x_sum(kind, j):
+        return x_copy(kind, j, stage.at[span(j, CHUNK)], recv.at[span(j, CHUNK)])
+
+    def x_rows(kind, j, buf):
+        here = buf.at[pl.ds(pl.multiple_of(x * ROWS + j * CHUNK, CHUNK), CHUNK)]
+        return x_copy(kind, j, here, here)
+
+    def hand_over(kind, before, s, value):
+        @pl.when(s < 2)
+        def _():
+            own[span(s, CHUNK), :] = value
+
+        @pl.when(s >= 2)
+        def _():
+            if before is not None:
+                x_sum(before, s - 2).wait_send()
+            stage[span(s - 2, CHUNK), :] = value.astype(BF)
+            x_sum(kind, s - 2).start()
+
+    serve_y(OUT)
+    serve_z(UP, (1,))
+    wait_weight(OUT)
+
+    def mix(i, carry):
+        s = lax.rem(i + 2, 4)
+        hand_over(X_MIX, None, s, contract(ctx[rows_of(s), :], w_out[...], 1, 0))
+        return carry
+
+    lax.fori_loop(0, 4, mix, 0)
+    serve_z(UP, (2, 3))
+    go_on(y_copy(DOWN, 0))
+
+    def row_of(row):
+        return vf[row:row + 1, :]
+
+    def normed(value):
+        centred = value - jnp.mean(value, axis=1, keepdims=True)
+        inverse = lax.rsqrt(jnp.mean(centred * centred, axis=1, keepdims=True) + NORM_EPS)
+        return centred * inverse, inverse
+
+    def norm_back(normal, inverse, grad):
+        first = jnp.mean(grad, axis=1, keepdims=True)
+        second = jnp.mean(grad * normal, axis=1, keepdims=True)
+        return inverse * (grad - first - normal * second)
+
+    def tiles(j, body):
+        def step(i, carry):
+            body(pl.ds(pl.multiple_of(j * CHUNK + i * TILE, TILE), TILE),
+                 pl.ds(pl.multiple_of(x * ROWS + j * CHUNK + i * TILE, TILE), TILE))
+            return carry
+        lax.fori_loop(0, CHUNK // TILE, step, 0)
+
+    def first_norm(r, g):
+        summed = xw[g, :].astype(F32) + own[r, :] + recv[r, :].astype(F32) + row_of(R_BO)
+        normal, inverse = normed(summed)
+        n1[r, :] = normal
+        inv1[r, :] = jnp.broadcast_to(inverse, (TILE, 128))
+        hw[g, :] = (normal * row_of(R_G1) + row_of(R_C1)).astype(BF)
+
+    for j in range(2):
+        x_sum(X_MIX, j).wait_recv()
+        tiles(j, first_norm)
+        x_rows(X_NORM, j, hw).start()
+
+    serve_y(UP)
+    serve_z(DOWN)
+    wait_weight(UP)
+
+    def arrived(kind, s, buf):
+        @pl.when(s >= 2)
+        def _():
+            there = buf.at[rows_of(s)]
+            x_copy(kind, s - 2, there, there).wait_recv()
+
+    def up_bias(n):
+        return vf[pl.ds(8 + n * 2 + x, 1), :]
+
+    def ffn_up(s, carry):
+        rows = rows_of(s)
+        arrived(X_NORM, s, hw)
+        for n in range(2):
+            pre = contract(hw[rows, :], w_up[:, n * 1024:(n + 1) * 1024], 1, 0) + up_bias(n)
+            cdf = 0.5 * (1.0 + lax.erf(pre * SQRT_HALF))
+            act[rows, n * 1024:(n + 1) * 1024] = (pre * cdf).astype(BF)
+            slope[rows, n * 1024:(n + 1) * 1024] = (
+                cdf + pre * INV_ROOT_TAU * jnp.exp(-0.5 * pre * pre)
+            ).astype(BF)
+        return carry
+
+    lax.fori_loop(0, 4, ffn_up, 0)
+    go_on(remote(cot.at[1 - y], cotb.at[span(y, CHUNK)], ys.at[Y_COT], yr.at[Y_COT], at_y))
+    serve_y(DOWN)
+    wait_weight(DOWN)
+
+    def ffn_down(i, carry):
+        s = lax.rem(i + 2, 4)
+        hand_over(X_FFN, X_MIX, s, contract(act[rows_of(s), :], w_down[...], 1, 0))
+        return carry
+
+    lax.fori_loop(0, 4, ffn_down, 0)
+
+    def bump(row, value):
+        acc[row] += fold_rows(value)
+
+    def second_norm(r, g):
+        h1 = n1[r, :] * row_of(R_G1) + row_of(R_C1)
+        normal, inverse = normed(h1 + own[r, :] + recv[r, :].astype(F32) + row_of(R_BD))
+        outb[r, :] = (normal * row_of(R_G2) + row_of(R_C2)).astype(BF)
+        dy = cotb[r, :].astype(F32)
+        bump(R_G2, dy * normal)
+        bump(R_C2, dy)
+        grad = norm_back(normal, inverse, dy * row_of(R_G2))
+        bump(R_BD, grad)
+        da[r, :] = grad
+        aw[g, :] = grad.astype(BF)
+
+    local_cot.wait()
+    cot_here = cotb.at[span(1 - y, CHUNK)]
+    remote(cot.at[1 - y], cot_here, ys.at[Y_COT], yr.at[Y_COT], at_y).wait_recv()
+    for j in range(2):
+        x_sum(X_FFN, j).wait_recv()
+        tiles(j, second_norm)
+        x_rows(X_DA2, j, aw).start()
+    out_here = pltpu.make_async_copy(outb.at[span(y, CHUNK)], out.at[y], os.at[0])
+    out_here.start()
+    go_on(remote(outb.at[span(1 - y, CHUNK)], out.at[y], ys.at[Y_OUT], yr.at[Y_OUT], at_y))
+
+    def ffn_back(s, carry):
+        rows = rows_of(s)
+        arrived(X_DA2, s, aw)
+        for n in range(2):
+            cols = slice(n * 1024, (n + 1) * 1024)
+            grad = contract(aw[rows, :], w_down[cols, :], 1, 1) * slope[rows, cols].astype(F32)
+            bump(R_BU + n, grad)
+            slope[rows, cols] = grad.astype(BF)
+        hand_over(X_DH, X_FFN, s, contract(slope[rows, :], w_up[...], 1, 1))
+        return carry
+
+    lax.fori_loop(0, 4, ffn_back, 0)
+
+    units = {
+        U_DOWN: (g_down, c_down, y_down, z_down, o_down, gd),
+        U_UP: (g_up, c_up, y_up, z_up, o_up, gu),
+        U_OUT: (g_out, c_out, y_out, z_out, o_out, go),
+        U_Q: tuple(r.at[0] for r in (g_qkv, c_qkv, y_qkv, z_qkv, o_qkv, gq)),
+        U_K: tuple(r.at[1] for r in (g_qkv, c_qkv, y_qkv, z_qkv, o_qkv, gq)),
+        U_V: tuple(r.at[2] for r in (g_qkv, c_qkv, y_qkv, z_qkv, o_qkv, gq)),
+    }
+
+    def core_copy(u):
+        g, rc = units[u][0], units[u][1]
+        return remote(g.at[1 - c], rc, gsc.at[u], grc.at[u], at_c)
+
+    def y_part(u):
+        g, ry = units[u][0], units[u][2]
+        return remote(g.at[c, 1 - y], ry, gsy.at[u], gry.at[u], at_y)
+
+    def z_part(u, k):
+        g, rz = units[u][0], units[u][3]
+        to = lax.rem(z + k, ZS)
+        return remote(g.at[c, y, to], rz.at[k - 1], gsz.at[u, k - 1], grz.at[u, k - 1], at_z[k - 1])
+
+    def add_pieces(g, yy, other):
+        for zz in range(ZS):
+            rows = g.shape[3]
+            def step(i, carry):
+                r = span(i, TILE)
+                g[c, yy, zz, r, :] = (
+                    g[c, yy, zz, r, :].astype(F32) + other[zz, r, :].astype(F32)
+                ).astype(BF)
+                return carry
+            lax.fori_loop(0, rows // TILE, step, 0)
+
+    def send_core(u):
+        go_on(core_copy(u))
+
+    def send_y(u):
+        g, rc = units[u][0], units[u][1]
+        core_copy(u).wait_recv()
+        add_pieces(g, 1 - y, rc.at[1 - y])
+        go_on(y_part(u))
+        add_pieces(g, y, rc.at[y])
+
+    def send_z(u):
+        g, ry = units[u][0], units[u][2]
+        y_part(u).wait_recv()
+        add_pieces(g, y, ry)
+        for k in range(1, ZS):
+            go_on(z_part(u, k))
+
+    finals = []
+
+    def finish(u):
+        g, _, _, rz, o, dest = units[u]
+        for k in range(1, ZS):
+            z_part(u, k).wait_recv()
+        rows = g.shape[3]
+        def step(i, carry):
+            r = span(i, TILE)
+            value = g[c, y, z, r, :].astype(F32)
+            for k in range(ZS - 1):
+                value = value + rz[k, r, :].astype(F32)
+            o[r, :] = value
+            return carry
+        lax.fori_loop(0, rows // TILE, step, 0)
+        copy = pltpu.make_async_copy(o, dest, os.at[1 + u])
+        copy.start()
+        finals.append(copy)
+
+    def grad_down(i, carry):
+        value = contract(act[:, span(i, 512)], aw[...], 0, 0).astype(BF)
+        for d in range(8):
+            g_down[d % 2, i // 2, d // 2, span(i % 2, 512), :] = value[:, d * 128:(d + 1) * 128]
+        return carry
+
+    lax.fori_loop(0, 4, grad_down, 0)
+    send_core(U_DOWN)
+
+    def grad_up(index, carry):
+        i, n = index // 2, index % 2
+        value = contract(hw[:, span(i, 512)], slope[:, span(n, 1024)], 0, 0).astype(BF)
+        for d in range(4):
+            g_up[d % 2, n, i * 2 + d // 2] = value[d * 128:(d + 1) * 128, :]
+        return carry
+
+    lax.fori_loop(0, 4, grad_up, 0)
+    send_core(U_UP)
+    send_y(U_DOWN)
+
+    def back_norm(r, g):
+        grad = da[r, :] + own[r, :] + recv[r, :].astype(F32)
+        normal = n1[r, :]
+        bump(R_G1, grad * normal)
+        bump(R_C1, grad)
+        grad = norm_back(normal, inv1[r, 0:1], grad * row_of(R_G1))
+        bump(R_BO, grad)
+        da[r, :] = grad
+        a1w[g, :] = grad.astype(BF)
+
+    for j in range(2):
+        x_sum(X_DH, j).wait_recv()
+        tiles(j, back_norm)
+        x_rows(X_DA1, j, a1w).start()
+
+    send_y(U_UP)
+
+    def ctx_back(s, carry):
+        rows = rows_of(s)
+        arrived(X_DA1, s, a1w)
+        dctx[rows, :] = contract(a1w[rows, :], w_out[...], 1, 1).astype(BF)
+        return carry
+
+    lax.fori_loop(0, 4, ctx_back, 0)
+
+    def attend_back(pair, carry):
+        lanes = span(pair, 128)
+        for t in range(2):
+            keys = pl.ds(t * 128, WINDOW)
+            query = two_blocks(qkv.at[0], t, lanes)
+            key, value = qkv[1, keys, lanes], qkv[2, keys, lanes]
+            grad = two_blocks(dctx, t, lanes)
+            product = grad.astype(F32) * two_blocks(ctx, t, lanes).astype(F32)
+            grad_q = jnp.zeros((ROWS, 128), F32)
+            grad_k = jnp.zeros((WINDOW, 128), F32)
+            grad_v = jnp.zeros((WINDOW, 128), F32)
+            for h, half in enumerate(halves):
+                grad_h = jnp.where(half, grad, none)
+                weight = prob[pair * 4 + t * 2 + h]
+                row_dot = jnp.sum(jnp.where(half, product, 0.0), axis=1, keepdims=True)
+                score = (weight.astype(F32) * (contract(grad_h, value, 1, 1) - row_dot)).astype(BF)
+                grad_q = grad_q + contract(score, jnp.where(half, key, none), 1, 0)
+                grad_k = grad_k + contract(score, jnp.where(half, query, none), 0, 0)
+                grad_v = grad_v + contract(weight, grad_h, 0, 0)
+            grad_q = grad_q * (HD ** -0.5)
+            acc[R_BQ, :, lanes] += fold_rows(grad_q)
+            acc[R_BV, :, lanes] += fold_rows(grad_v)
+            grad_q = grad_q.astype(BF)
+            qkv[0, t * 128:t * 128 + 128, lanes] = grad_q[:128]
+            qkv[0, t * 128 + 256:t * 128 + 384, lanes] = grad_q[128:]
+            if t == 0:
+                acc_k[0:WINDOW, :] = grad_k
+                acc_v[0:WINDOW, :] = grad_v
+                acc_k[WINDOW:SEQ, :] = jnp.zeros((128, 128), F32)
+                acc_v[WINDOW:SEQ, :] = jnp.zeros((128, 128), F32)
+            else:
+                for i, total, more in ((1, acc_k, grad_k), (2, acc_v, grad_v)):
+                    qkv[i, 0:128, lanes] = total[0:128, :].astype(BF)
+                    qkv[i, 128:SEQ, lanes] = (total[128:SEQ, :] + more).astype(BF)
+        return carry
+
+    lax.fori_loop(0, 4, attend_back, 0)
+
+    def input_back(i, carry):
+        s = lax.rem(i + 2, 4)
+        rows = rows_of(s)
+        value = contract(qkv[0, rows, :], w_qkv[0], 1, 1)
+        value = value + contract(qkv[1, rows, :], w_qkv[1], 1, 1)
+        value = value + contract(qkv[2, rows, :], w_qkv[2], 1, 1)
+        hand_over(X_DX, X_DH, s, value)
+        return carry
+
+    lax.fori_loop(0, 4, input_back, 0)
+
+    def grad_qkv(index, carry):
+        kind, i = index // 2, index % 2
+        value = contract(xw[:, span(i, 512)], qkv[kind], 0, 0).astype(BF)
+        for d in range(4):
+            for yy in range(2):
+                g_qkv[kind, d % 2, yy, i * 2 + d // 2] = (
+                    value[d * 128:(d + 1) * 128, yy * 256:(yy + 1) * 256]
+                )
+        return carry
+
+    def grad_out():
+        value = contract(ctx[...], a1w[...], 0, 0).astype(BF)
+        for d in range(8):
+            for yy in range(2):
+                g_out[d % 2, yy, d // 2] = value[yy * 256:(yy + 1) * 256, d * 128:(d + 1) * 128]
+
+    grad_out()
+    send_core(U_OUT)
+    for kind, u in ((0, U_Q), (1, U_K), (2, U_V)):
+        lax.fori_loop(kind * 2, kind * 2 + 2, grad_qkv, 0)
+        send_core(u)
+
+    def vec_piece(d):
+        return vg.at[d % 2, d // 2]
+
+    for row in range(2, 8):
+        line = jnp.sum(acc[row], axis=0, keepdims=True)
+        for d in range(8):
+            vg[d % 2, d // 2, row:row + 1, :] = line[:, d * 128:(d + 1) * 128]
+    for n in range(2):
+        line = jnp.sum(acc[R_BU + n], axis=0, keepdims=True)
+        for d in range(8):
+            vg[d % 2, d // 2, pl.ds(8 + n * 2 + x, 1), :] = line[:, d * 128:(d + 1) * 128]
+    for row, source in ((0, R_BQ), (1, R_BV)):
+        line = jnp.sum(acc[source], axis=0, keepdims=True)
+        for yy in range(2):
+            for half in range(2):
+                vg[half, 2 * yy + x, row:row + 1, :] = (
+                    line[:, yy * 256 + half * 128:yy * 256 + (half + 1) * 128]
+                )
+    vec_x = remote(vg, vgx, vs.at[0], vr.at[0], at_x)
+    vec_c = remote(vg.at[1 - c], vgc, vs.at[1], vr.at[1], at_c)
+    vec_y = remote(vg.at[c], vgy, vs.at[2], vr.at[2], at_y)
+
+    def vec_z(k):
+        to = lax.rem(z + k, ZS)
+        return remote(vg.at[c, to], vgz.at[k - 1], vs.at[2 + k], vr.at[2 + k], at_z[k - 1])
+
+    vec_x.start()
+    send_y(U_OUT)
+    send_z(U_DOWN)
+    send_y(U_Q)
+    vec_x.wait()
+    vg[...] = vg[...] + vgx[...]
+    vec_c.start()
+    send_y(U_K)
+    send_y(U_V)
+    vec_c.wait()
+    vg[c] = vg[c] + vgc[...]
+    vec_y.start()
+    send_z(U_UP)
+
+    def last_sum(j, other):
+        x_sum(X_DX, j).wait_recv()
+
+        def body(r, g):
+            value = da[r, :] + own[r, :] + recv[r, :].astype(F32)
+            if other:
+                gts[pl.ds(pl.multiple_of(r.start - j * CHUNK, TILE), TILE), :] = value.astype(BF)
+            else:
+                da[r, :] = value
+        tiles(j, body)
+
+    last_sum(1 - y, True)
+    go_on(remote(gts, gtr, ys.at[Y_GTOK], yr.at[Y_GTOK], at_y))
+    last_sum(y, False)
+    gtok_here = pltpu.make_async_copy(da.at[span(y, CHUNK)], gtok.at[y], os.at[7])
+    gtok_here.start()
+    vec_y.wait()
+    vg[c] = vg[c] + vgy[...]
+    for k in range(1, ZS):
+        vec_z(k).start()
+    send_z(U_OUT)
+    send_z(U_Q)
+    send_z(U_K)
+    send_z(U_V)
+    finish(U_DOWN)
+    finish(U_UP)
+    for k in range(1, ZS):
+        vec_z(k).wait()
+    gvb[...] = vg[c, z] + vgz[0] + vgz[1] + vgz[2]
+    vec_here = pltpu.make_async_copy(gvb.at[0:12], gv, os.at[8])
+    vec_here.start()
+    remote(gts, gtr, ys.at[Y_GTOK], yr.at[Y_GTOK], at_y).wait_recv()
+    gtf[...] = gtr[...].astype(F32)
+    gtok_there = pltpu.make_async_copy(gtf, gtok.at[1 - y], os.at[9])
+    gtok_there.start()
+    finish(U_OUT)
+    finish(U_Q)
+    finish(U_K)
+    finish(U_V)
+    remote(outb.at[span(1 - y, CHUNK)], out.at[1 - y], ys.at[Y_OUT], yr.at[Y_OUT], at_y).wait_recv()
+    for kind, buf in ((X_NORM, hw), (X_DA2, aw), (X_DA1, a1w)):
+        for j in range(2):
+            x_rows(kind, j, buf).wait_send()
+    for j in range(2):
+        x_sum(X_DX, j).wait_send()
+    for copy in sent:
+        copy.wait_send()
+    for copy in finals + [out_here, gtok_here, gtok_there, vec_here]:
+        copy.wait()
+
+
+def layer(tokens, segment_ids, w_qkv, w_out, w_up, w_down, vectors, cotangent):
+    vmem, dma = pltpu.VMEM, pltpu.SemaphoreType.DMA
+    outs = (
+        jax.ShapeDtypeStruct(tokens.shape, BF),
+        jax.ShapeDtypeStruct(tokens.shape, F32),
+        jax.ShapeDtypeStruct(w_qkv.shape, F32),
+        jax.ShapeDtypeStruct(w_out.shape, F32),
+        jax.ShapeDtypeStruct(w_up.shape, F32),
+        jax.ShapeDtypeStruct(w_down.shape, F32),
+        jax.ShapeDtypeStruct(vectors.shape, F32),
+    )
+    pieces = ((1024, 128), (128, 1024), (256, 128), (128, 256))
+    lead = ((), (), (), (3,))
+    scratch = [
+        vmem((3, D, COLS), BF), vmem((COLS, D), BF), vmem((D, HID), BF), vmem((HID, D), BF),
+        vmem((8, 12, 128), BF), vmem((16, D), F32),
+    ]
+    for shape in ((2, 2, 4), (2, 4), (4,), (3,)):
+        scratch += [vmem(first + shape + piece, BF) for first, piece in zip(lead, pieces)]
+    scratch += [vmem((3, 128, 256), F32), vmem((256, 128), F32), vmem((128, 1024), F32), vmem((1024, 128), F32)]
+    scratch += [
+        vmem((SEQ, D), BF), vmem((3, SEQ, COLS), BF), vmem((SEQ, COLS), BF),
+        vmem((16, ROWS, WINDOW), BF), vmem((2, ROWS, WINDOW), F32), vmem((SEQ, D), BF),
+        vmem((SEQ, HID), BF), vmem((SEQ, HID), BF), vmem((SEQ, D), BF), vmem((SEQ, D), BF),
+        vmem((SEQ, COLS), BF),
+        vmem((ROWS, D), F32), vmem((ROWS, D), F32), vmem((ROWS, D), F32), vmem((ROWS, 128), F32),
+        vmem((ROWS, D), BF), vmem((ROWS, D), BF), vmem((ROWS, D), BF), vmem((ROWS, D), BF),
+        vmem((CHUNK, D), BF), vmem((CHUNK, D), BF), vmem((CHUNK, D), F32),
+        vmem((12, 8, D), F32),
+        vmem((2, 4, 16, 128), F32), vmem((2, 4, 16, 128), F32), vmem((4, 16, 128), F32),
+        vmem((4, 16, 128), F32), vmem((3, 16, 128), F32), vmem((16, 128), F32),
+        vmem((SEQ, 128), F32), vmem((SEQ, 128), F32),
+        dma((5, 3)), dma((5, 3)), dma((4, 4)), dma((4, 4)), dma((5, 8)), dma((5, 8)),
+        dma((8, 2)), dma((8, 2)), dma((4,)), dma((4,)),
+        dma((6,)), dma((6,)), dma((6,)), dma((6,)), dma((6, 3)), dma((6, 3)),
+        dma((6,)), dma((6,)), dma((7,)), dma((10,)),
+    ]
+    hbm = pl.BlockSpec(memory_space=pl.ANY)
+    return pl.pallas_call(
+        layer_kernel,
+        out_shape=outs,
+        in_specs=[hbm, pl.BlockSpec(memory_space=pltpu.VMEM)] + [hbm] * 6,
+        out_specs=[hbm] * 7,
+        scratch_shapes=scratch,
+        compiler_params=pltpu.CompilerParams(
+            collective_id=0, has_side_effects=True, vmem_limit_bytes=67043328
+        ),
+    )(tokens, segment_ids, w_qkv, w_out, w_up, w_down, vectors, cotangent)
+
+
 def solution(mesh):
+    step = layer if (mesh.shape["dp"], mesh.shape["tensor"]) == (8, 4) else body
     return jax.shard_map(
-        body,
+        step,
         mesh=mesh,
         in_specs=(
             P("dp", "tensor", None),

time: 944 us -> 246 us (0.26)
  the two profiles are of different devices: /device:TPU:0 before, /device:TPU:25 now
where the time goes in v1:
time: 246 us
  Pallas kernels  238 us (97%)
  local copies, waits for them, and re-layouts  7.47 us (3%)
    pallas_call x1, Pallas kernels, layer(): pl.pallas_call(layer_kernel, out_shape=outs, in_specs=[hbm, pl.BlockSpec(...  238 us
    unnamed x19, local copies, waits for them, and re-layouts  7.47 us

profile of v1, /device:TPU:25, one launch (start us, length us, event | category | flops | bytes accessed | tf_op | source)
XLA Modules:
  0.0 246.0 jit_solution(6549801169039722661)
XLA Ops:
  0.6 237.8 %shard_map.135 = (bf16[2,128,1024]{2,1,0:T(8,128)(2,1)}, f32[2,128,1024]{2,1,0:T(8,128)}, f32[3,128,256]{2,1,0:T(8,128)}, f32[256,128]{1,0:T(8,128)}, f32[128,10...) custom-call(bf16[2,128,1024]{2,1,0:T(8,128)(2,1)} %tok.1, s32[2,512]{1,0:T(2,128)} %seg.1, ...), custom_call_target="tpu_custom_call" | custom-call | tf_op jit(solution)/shard_map/pallas_call | solution.py:956
  238.5 0.0 copy-start
  238.5 2.0 copy.22
  240.4 0.0 copy-done
  240.4 0.0 copy-start.3
  240.4 1.0 copy.23
  241.4 0.3 copy-done.3
  241.7 0.0 copy-start.4
  241.7 0.0 copy-start.2
  241.7 0.7 copy.24
  242.4 0.2 copy-done.4
  242.7 0.7 copy.25
  243.3 0.0 copy-done.2
  243.3 0.0 copy-start.1
  243.3 0.8 copy.26
  244.1 0.4 copy-done.1
  244.6 0.0 copy-start.5
  244.6 0.8 copy.27
  245.4 0.0 copy-done.5
  245.4 0.6 copy.28
Async XLA Ops:
  238.5 2.0 copy-start
  240.4 1.2 copy-start.3
  241.7 1.0 copy-start.4
  241.7 1.7 copy-start.2
  243.3 1.2 copy-start.1
  244.6 0.8 copy-start.5

commit v2 on v1

--- a/solution.py
+++ b/solution.py
@@ -265,7 +265,9 @@
 
 Y_TOK, Y_COT, Y_OUT, Y_GTOK = range(4)
 X_TOK, X_MIX, X_NORM, X_FFN, X_DA2, X_DH, X_DA1, X_DX = range(8)
-QKV, OUT, UP, DOWN, VEC = range(5)
+W_Q, W_K, W_V, W_OUT, W_UP, W_DOWN, W_VEC = range(7)
+Y_FIRST = (W_Q, W_OUT)
+Z_FIRST = (0,)
 U_DOWN, U_UP, U_OUT, U_V, U_K, U_Q = range(6)
 R_BQ, R_BV, R_BO, R_G1, R_C1, R_BD, R_G2, R_C2, R_BU = range(9)
 ZS = 4
@@ -301,6 +303,7 @@
     c_down, c_up, c_out, c_qkv,
     y_down, y_up, y_out, y_qkv,
     z_down, z_up, z_out, z_qkv,
+    h_down, h_up, h_out, h_qkv,
     o_qkv, o_out, o_up, o_down,
     xw, qkv, ctx, prob, bias, hw, act, slope, aw, a1w, dctx,
     own, n1, da, inv1, recv, stage, cotb, outb, gts, gtr, gtf,
@@ -315,7 +318,6 @@
     at_x = {"dp": dp, "tensor": y * 2 + (1 - x)}
     at_y = {"dp": dp, "tensor": (1 - y) * 2 + x}
     at_c = {"dp": z * 2 + (1 - c), "tensor": tensor}
-    at_z = [{"dp": lax.rem(z + k, ZS) * 2 + c, "tensor": tensor} for k in range(1, ZS)]
 
     def remote(src, dst, send, recv_sem, where):
         return pltpu.make_async_remote_copy(
@@ -324,7 +326,7 @@
         )
 
     barrier = pltpu.get_barrier_semaphore()
-    for where in [at_x, at_y, at_c] + at_z:
+    for where in [at_x, at_y, at_c] + [{"dp": lax.rem(z + k, ZS) * 2 + c, "tensor": tensor} for k in range(1, ZS)]:
         pl.semaphore_signal(barrier, inc=1, device_id=where, device_id_type=MESH)
     pl.semaphore_wait(barrier, 6)
 
@@ -334,72 +336,88 @@
         copy.start()
         sent.append(copy)
 
-    args = [wq, wo, wu, wd, vec]
+    args = [wq.at[0], wq.at[1], wq.at[2], wo, wu, wd, vec]
+    edge = jnp.logical_or(z == 0, z == ZS - 1)
+    middle = jnp.logical_not(edge)
+    later = []
+
+    def z_device(where):
+        return {"dp": where * 2 + c, "tensor": tensor}
+
+    def go_if(condition, copy):
+        @pl.when(condition)
+        def _():
+            copy.start()
+        later.append((condition, copy))
 
     def place(m, yy, d):
-        if m == QKV:
-            return w_qkv.at[:, span(d, 128), span(yy, 256)]
-        if m == OUT:
+        if m <= W_V:
+            return w_qkv.at[m, span(d, 128), span(yy, 256)]
+        if m == W_OUT:
             return w_out.at[span(yy, 256), span(d, 128)]
-        if m == UP:
+        if m == W_UP:
             return w_up.at[span(d, 128), span(yy, 1024)]
-        if m == DOWN:
+        if m == W_DOWN:
             return w_down.at[span(yy, 1024), span(d, 128)]
         return w_vec.at[d]
 
     def from_z(k):
         return lax.rem(z + ZS - k, ZS)
 
-    def z_copy(m, k):
-        return remote(args[m], place(m, y, dp), wsz.at[m, k - 1], wrz.at[m, k - 1], at_z[k - 1])
-
-    def z_arrived(m, k):
-        here = place(m, y, from_z(k) * 2 + c)
-        remote(args[m], here, wsz.at[m, k - 1], wrz.at[m, k - 1], at_z[k - 1]).wait_recv()
-
-    def y_copy(m, j):
-        if j == 0:
-            return remote(args[m], place(m, y, dp), wsy.at[m, 0], wry.at[m, 0], at_y)
-        here = place(m, y, from_z(j) * 2 + c)
-        return remote(here, here, wsy.at[m, j], wry.at[m, j], at_y)
-
-    def y_place(m, j):
-        return place(m, 1 - y, (z if j == 0 else from_z(j)) * 2 + c)
-
-    def y_arrived(m, j):
-        here = y_place(m, j)
-        remote(here, here, wsy.at[m, j], wry.at[m, j], at_y).wait_recv()
-
-    def c_copy(m, j):
-        if j == 0:
-            return remote(args[m], place(m, y, dp), wsc.at[m, 0], wrc.at[m, 0], at_c)
-        here = place(m, y, from_z(j) * 2 + c) if j < 4 else y_place(m, j - 4)
-        return remote(here, here, wsc.at[m, j], wrc.at[m, j], at_c)
-
-    def c_arrived(m, j):
-        d = (z if j == 0 or j == 4 else from_z(j % 4)) * 2 + 1 - c
-        here = place(m, y if j < 4 else 1 - y, d)
-        remote(here, here, wsc.at[m, j], wrc.at[m, j], at_c).wait_recv()
-
-    def serve_z(m, ks=(1, 2, 3)):
-        for k in ks:
-            z_arrived(m, k)
-            if m != VEC:
-                go_on(y_copy(m, k))
-            go_on(c_copy(m, k))
-
-    def serve_y(m):
-        for j in range(4):
-            y_arrived(m, j)
-            go_on(c_copy(m, j + 4))
+    def column(r):
+        return y if r == 0 else 1 - y
+
+    def z_send(m, r):
+        source = args[m] if r == 0 else place(m, 1 - y, dp)
+        for k, there in ((1, z != ZS - 1), (3, z != 0), (2, None)):
+            there = None if m == W_VEC else there
+            copy = remote(
+                source, place(m, column(r), dp), wsz.at[m, r, k - 1], wrz.at[m, r, k - 1],
+                z_device(lax.rem(z + k, ZS)),
+            )
+            if there is None:
+                go_on(copy)
+            else:
+                go_if(there, copy)
+
+    def z_serve(m, r, step):
+        k = (jnp.where(z == 0, 3, 1), 2, jnp.where(z == 0, 1, 3))[step]
+        here = place(m, column(r), from_z(k) * 2 + c)
+        remote(here, here, wsz.at[m, r, k - 1], wrz.at[m, r, k - 1], at_x).wait_recv()
+        if step == 1 and m != W_VEC:
+            slot = jnp.where(z == 1, 0, 2)
+            go_if(middle, remote(
+                here, here, wsz.at[m, r, 3], wrz.at[m, r, slot], z_device(jnp.where(z == 1, 0, 3)),
+            ))
+        if r == 0 and m not in Y_FIRST and m != W_VEC:
+            go_on(remote(here, here, wsy.at[m, k], wry.at[m, from_z(k)], at_y))
+        c_send(m, here)
+
+    def y_send(m):
+        go_on(remote(args[m], place(m, y, dp), wsy.at[m, 0], wry.at[m, z], at_y))
+
+    def y_serve(m, step):
+        zz = lax.rem(z + step, ZS)
+        here = place(m, 1 - y, zz * 2 + c)
+        remote(here, here, wsy.at[m, 0], wry.at[m, zz], at_y).wait_recv()
+        c_send(m, here)
+
+    def c_send(m, source, dest=None):
+        dest = source if dest is None else dest
+        remote(source, dest, wsc.at[m], wrc.at[m], at_c).start()
+
+    def own_send(m):
+        c_send(m, args[m], place(m, y, dp))
+        pltpu.make_async_copy(args[m], place(m, y, dp), ls.at[m]).start()
+
+    def half_of(m):
+        if m <= W_V:
+            return w_qkv.at[m, :, 0:256]
+        return (w_out.at[0:256], w_up.at[:, 0:1024], w_down.at[0:1024], w_vec.at[0:4])[m - W_OUT]
 
     def wait_weight(m):
-        if m != VEC:
-            pltpu.make_async_copy(args[m], place(m, y, dp), ls.at[m]).wait()
-        else:
-            pltpu.make_async_copy(args[m], place(m, y, dp), ls.at[m]).wait()
-        for j in range(4 if m == VEC else 8):
-            c_arrived(m, j)
+        pltpu.make_async_copy(args[m], place(m, y, dp), ls.at[m]).wait()
+        remote(half_of(m), half_of(m), wsc.at[m], wrc.at[m], at_c).wait_recv()
 
     def x_copy(kind, j, src, dst):
         return remote(src, dst, xs.at[kind, j], xr.at[kind, j], at_x)
@@ -407,19 +425,18 @@
     def tok_rows(xx, yy):
         return pl.ds(pl.multiple_of(xx * ROWS + yy * CHUNK, CHUNK), CHUNK)
 
-    y_tok = remote(tok.at[1 - y], xw.at[tok_rows(x, y)], ys.at[Y_TOK], yr.at[Y_TOK], at_y)
-    go_on(y_tok)
+    for m in (W_Q, W_K, W_V):
+        y_send(m)
+        z_send(m, 0)
+    y_send(W_OUT)
+    go_on(remote(tok.at[1 - y], xw.at[tok_rows(x, y)], ys.at[Y_TOK], yr.at[Y_TOK], at_y))
     go_on(x_copy(X_TOK, 0, tok.at[y], xw.at[tok_rows(x, y)]))
-    local_x = pltpu.make_async_copy(tok.at[y], xw.at[tok_rows(x, y)], ls.at[5])
+    z_send(W_VEC, 0)
+    for m in range(7):
+        own_send(m)
+    local_x = pltpu.make_async_copy(tok.at[y], xw.at[tok_rows(x, y)], ls.at[7])
     local_x.start()
-    for m in (QKV, VEC, OUT, UP, DOWN):
-        for k in range(1, ZS):
-            go_on(z_copy(m, k))
-        if m == QKV:
-            go_on(y_copy(m, 0))
-        go_on(c_copy(m, 0))
-        pltpu.make_async_copy(args[m], place(m, y, dp), ls.at[m]).start()
-    local_cot = pltpu.make_async_copy(cot.at[y], cotb.at[span(y, CHUNK)], ls.at[6])
+    local_cot = pltpu.make_async_copy(cot.at[y], cotb.at[span(y, CHUNK)], ls.at[8])
     local_cot.start()
 
     seg_row = seg[pl.ds(y, 1), :].astype(F32)
@@ -434,25 +451,41 @@
     acc[...] = jnp.zeros_like(acc)
     vg[...] = jnp.zeros_like(vg)
 
+    y_serve(W_Q, 0)
+    z_send(W_Q, 1)
+    y_serve(W_OUT, 0)
+    for step in range(2):
+        for m in (W_K, W_V, W_Q):
+            z_serve(m, 0, step)
+    z_send(W_OUT, 0)
+    z_send(W_OUT, 1)
     y_tok_here = xw.at[tok_rows(x, 1 - y)]
     remote(tok.at[1 - y], y_tok_here, ys.at[Y_TOK], yr.at[Y_TOK], at_y).wait_recv()
     go_on(x_copy(X_TOK, 1, y_tok_here, y_tok_here))
-    serve_z(QKV)
-    serve_z(VEC)
-    go_on(y_copy(OUT, 0))
-    serve_z(OUT)
-    go_on(y_copy(UP, 0))
-    serve_y(QKV)
-    wait_weight(VEC)
+    z_serve(W_Q, 1, 0)
+    z_serve(W_Q, 1, 1)
+    for m in (W_K, W_V, W_Q):
+        z_serve(m, 0, 2)
+    z_serve(W_Q, 1, 2)
+    z_send(W_UP, 0)
+    y_send(W_UP)
+    for r in range(2):
+        for step in range(2):
+            z_serve(W_OUT, r, step)
+    for step in range(3):
+        z_serve(W_VEC, 0, step)
+    for step in range(4):
+        y_serve(W_K, step)
+        y_serve(W_V, step)
+    wait_weight(W_VEC)
     for d in range(8):
         vf[0:12, d * 128:(d + 1) * 128] = w_vec[d].astype(F32)
     local_x.wait()
     for j, yy in ((0, y), (1, 1 - y)):
         there = xw.at[tok_rows(1 - x, yy)]
         x_copy(X_TOK, j, there, there).wait_recv()
-    wait_weight(QKV)
-
-    zero_bias = jnp.zeros((1, COLS), F32)
+    for m in (W_Q, W_K, W_V):
+        wait_weight(m)
 
     def head_bias(row):
         parts = [vf[row:row + 1, pl.ds(pl.multiple_of(yy * 512 + x * 256, 256), 256)] for yy in range(2)]
@@ -493,7 +526,15 @@
         ctx[span(t + 2, 128), lanes] = total[128:]
         return carry
 
-    lax.fori_loop(0, 8, attend, 0)
+    z_serve(W_UP, 0, 0)
+    lax.fori_loop(0, 4, attend, 0)
+    z_serve(W_UP, 0, 1)
+    z_send(W_DOWN, 0)
+    z_serve(W_OUT, 0, 2)
+    z_serve(W_OUT, 1, 2)
+    lax.fori_loop(4, 8, attend, 0)
+    z_serve(W_UP, 0, 2)
+    y_send(W_DOWN)
 
     def rows_of(s):
         mine = jnp.where(s < 2, x, 1 - x)
@@ -518,9 +559,7 @@
             stage[span(s - 2, CHUNK), :] = value.astype(BF)
             x_sum(kind, s - 2).start()
 
-    serve_y(OUT)
-    serve_z(UP, (1,))
-    wait_weight(OUT)
+    wait_weight(W_OUT)
 
     def mix(i, carry):
         s = lax.rem(i + 2, 4)
@@ -528,8 +567,9 @@
         return carry
 
     lax.fori_loop(0, 4, mix, 0)
-    serve_z(UP, (2, 3))
-    go_on(y_copy(DOWN, 0))
+    z_serve(W_DOWN, 0, 0)
+    y_serve(W_UP, 0)
+    y_serve(W_UP, 1)
 
     def row_of(row):
         return vf[row:row + 1, :]
@@ -563,9 +603,10 @@
         tiles(j, first_norm)
         x_rows(X_NORM, j, hw).start()
 
-    serve_y(UP)
-    serve_z(DOWN)
-    wait_weight(UP)
+    z_serve(W_DOWN, 0, 1)
+    y_serve(W_UP, 2)
+    y_serve(W_UP, 3)
+    wait_weight(W_UP)
 
     def arrived(kind, s, buf):
         @pl.when(s >= 2)
@@ -588,10 +629,13 @@
             ).astype(BF)
         return carry
 
-    lax.fori_loop(0, 4, ffn_up, 0)
+    lax.fori_loop(0, 2, ffn_up, 0)
+    z_serve(W_DOWN, 0, 2)
+    lax.fori_loop(2, 4, ffn_up, 0)
     go_on(remote(cot.at[1 - y], cotb.at[span(y, CHUNK)], ys.at[Y_COT], yr.at[Y_COT], at_y))
-    serve_y(DOWN)
-    wait_weight(DOWN)
+    for step in range(4):
+        y_serve(W_DOWN, step)
+    wait_weight(W_DOWN)
 
     def ffn_down(i, carry):
         s = lax.rem(i + 2, 4)
@@ -640,73 +684,143 @@
     lax.fori_loop(0, 4, ffn_back, 0)
 
     units = {
-        U_DOWN: (g_down, c_down, y_down, z_down, o_down, gd),
-        U_UP: (g_up, c_up, y_up, z_up, o_up, gu),
-        U_OUT: (g_out, c_out, y_out, z_out, o_out, go),
-        U_Q: tuple(r.at[0] for r in (g_qkv, c_qkv, y_qkv, z_qkv, o_qkv, gq)),
-        U_K: tuple(r.at[1] for r in (g_qkv, c_qkv, y_qkv, z_qkv, o_qkv, gq)),
-        U_V: tuple(r.at[2] for r in (g_qkv, c_qkv, y_qkv, z_qkv, o_qkv, gq)),
+        U_DOWN: (g_down, c_down, y_down, z_down, h_down, o_down, gd),
+        U_UP: (g_up, c_up, y_up, z_up, h_up, o_up, gu),
+        U_OUT: (g_out, c_out, y_out, z_out, h_out, o_out, go),
     }
+    for u, i in ((U_Q, 0), (U_K, 1), (U_V, 2)):
+        units[u] = tuple(r.at[i] for r in (g_qkv, c_qkv, y_qkv, z_qkv, h_qkv, o_qkv, gq))
+
+    def piece_loop(rows, body):
+        size = min(rows, CHUNK)
+
+        def step(i, carry):
+            body(span(i, size))
+            return carry
+        lax.fori_loop(0, rows // size, step, 0)
+
+    def add_piece(g, yy, zz, other):
+        def body(r):
+            g[c, yy, zz, r, :] = (g[c, yy, zz, r, :].astype(F32) + other[r, :].astype(F32)).astype(BF)
+        piece_loop(g.shape[3], body)
 
     def core_copy(u):
         g, rc = units[u][0], units[u][1]
         return remote(g.at[1 - c], rc, gsc.at[u], grc.at[u], at_c)
 
-    def y_part(u):
+    def core_send(u):
+        go_on(core_copy(u))
+
+    def core_add(u, r):
+        g, rc = units[u][0], units[u][1]
+        for zz in range(ZS):
+            add_piece(g, column(r), zz, rc.at[column(r), zz])
+
+    def rs_y_copy(u):
         g, ry = units[u][0], units[u][2]
-        return remote(g.at[c, 1 - y], ry, gsy.at[u], gry.at[u], at_y)
-
-    def z_part(u, k):
+        source = g.at[c, 1 - y, pl.ds(z, 1)] if u in Z_FIRST else g.at[c, 1 - y]
+        return remote(source, ry, gsy.at[u], gry.at[u], at_y)
+
+    def rs_z_copy(u, r, k):
         g, rz = units[u][0], units[u][3]
         to = lax.rem(z + k, ZS)
-        return remote(g.at[c, y, to], rz.at[k - 1], gsz.at[u, k - 1], grz.at[u, k - 1], at_z[k - 1])
-
-    def add_pieces(g, yy, other):
+        return remote(g.at[c, column(r), to], rz.at[r, k - 1], gsz.at[u, r, k - 1], grz.at[u, r, k - 1], z_device(to))
+
+    def rs_hand_on(u, r):
+        g, rh = units[u][0], units[u][4]
+        far = jnp.where(z == 0, ZS - 1, 0)
+        return remote(g.at[c, column(r), far], rh.at[r], gsz.at[u, r, 3], grz.at[u, r, 3], z_device(jnp.where(z == 0, 1, 2)))
+
+    def z_hand_on(u, r):
+        go_if(edge, rs_hand_on(u, r))
+
+    def z_begin(u, r):
+        go_if(z != ZS - 1, rs_z_copy(u, r, 1))
+        go_if(z != 0, rs_z_copy(u, r, 3))
+        go_if(edge, rs_z_copy(u, r, 2))
+
+    def z_relay(u, r):
+        g, rh = units[u][0], units[u][4]
+
+        @pl.when(middle)
+        def _():
+            rs_hand_on(u, r).wait_recv()
+            add_piece(g, column(r), lax.rem(z + 2, ZS), rh.at[r])
+        go_if(middle, rs_z_copy(u, r, 2))
+
+    def start(u):
+        core_copy(u).wait_recv()
+        core_add(u, 1)
+        if u in Z_FIRST:
+            z_hand_on(u, 1)
+            core_add(u, 0)
+            z_hand_on(u, 0)
+            z_begin(u, 1)
+            z_begin(u, 0)
+        else:
+            go_on(rs_y_copy(u))
+            core_add(u, 0)
+
+    def y_to_z(u):
+        g, ry = units[u][0], units[u][2]
+        rs_y_copy(u).wait_recv()
         for zz in range(ZS):
-            rows = g.shape[3]
-            def step(i, carry):
-                r = span(i, TILE)
-                g[c, yy, zz, r, :] = (
-                    g[c, yy, zz, r, :].astype(F32) + other[zz, r, :].astype(F32)
-                ).astype(BF)
-                return carry
-            lax.fori_loop(0, rows // TILE, step, 0)
-
-    def send_core(u):
-        go_on(core_copy(u))
-
-    def send_y(u):
-        g, rc = units[u][0], units[u][1]
-        core_copy(u).wait_recv()
-        add_pieces(g, 1 - y, rc.at[1 - y])
-        go_on(y_part(u))
-        add_pieces(g, y, rc.at[y])
-
-    def send_z(u):
-        g, ry = units[u][0], units[u][2]
-        y_part(u).wait_recv()
-        add_pieces(g, y, ry)
-        for k in range(1, ZS):
-            go_on(z_part(u, k))
+            add_piece(g, y, zz, ry.at[zz])
+        z_hand_on(u, 0)
+        z_begin(u, 0)
+
+    def wait_z(u, r):
+        rs_z_copy(u, r, 2).wait_recv()
+
+        @pl.when(z != 0)
+        def _():
+            rs_z_copy(u, r, 1).wait_recv()
+
+        @pl.when(z != ZS - 1)
+        def _():
+            rs_z_copy(u, r, 3).wait_recv()
+
+    def z_total(u, r, rows):
+        g, rz = units[u][0], units[u][3]
+        value = g[c, column(r), z, rows, :].astype(F32)
+        for k in range(ZS - 1):
+            value = value + rz[r, k, rows, :].astype(F32)
+        return value
+
+    def z_to_y(u):
+        g = units[u][0]
+        wait_z(u, 1)
+
+        def body(rows):
+            g[c, 1 - y, z, rows, :] = z_total(u, 1, rows).astype(BF)
+        piece_loop(g.shape[3], body)
+        go_on(rs_y_copy(u))
 
     finals = []
 
     def finish(u):
-        g, _, _, rz, o, dest = units[u]
-        for k in range(1, ZS):
-            z_part(u, k).wait_recv()
-        rows = g.shape[3]
-        def step(i, carry):
-            r = span(i, TILE)
-            value = g[c, y, z, r, :].astype(F32)
-            for k in range(ZS - 1):
-                value = value + rz[k, r, :].astype(F32)
-            o[r, :] = value
-            return carry
-        lax.fori_loop(0, rows // TILE, step, 0)
+        g, _, ry, _, _, o, dest = units[u]
+        wait_z(u, 0)
+        if u in Z_FIRST:
+            rs_y_copy(u).wait_recv()
+
+        def body(rows):
+            value = z_total(u, 0, rows)
+            if u in Z_FIRST:
+                value = value + ry[0, rows, :].astype(F32)
+            o[rows, :] = value
+        piece_loop(g.shape[3], body)
         copy = pltpu.make_async_copy(o, dest, os.at[1 + u])
         copy.start()
         finals.append(copy)
+
+    for u in units:
+        for r in range(2 if u in Z_FIRST else 1):
+            for k, alone in ((1, z == 0), (3, z == ZS - 1)):
+                @pl.when(alone)
+                def _(u=u, r=r, k=k):
+                    rz = units[u][3]
+                    rz[r, k - 1] = jnp.zeros(rz.shape[2:], BF)
 
     def grad_down(i, carry):
         value = contract(act[:, span(i, 512)], aw[...], 0, 0).astype(BF)
@@ -715,7 +829,7 @@
         return carry
 
     lax.fori_loop(0, 4, grad_down, 0)
-    send_core(U_DOWN)
+    core_send(U_DOWN)
 
     def grad_up(index, carry):
         i, n = index // 2, index % 2
@@ -725,8 +839,9 @@
         return carry
 
     lax.fori_loop(0, 4, grad_up, 0)
-    send_core(U_UP)
-    send_y(U_DOWN)
+    core_send(U_UP)
+    start(U_DOWN)
+    start(U_UP)
 
     def back_norm(r, g):
         grad = da[r, :] + own[r, :] + recv[r, :].astype(F32)
@@ -743,7 +858,8 @@
         tiles(j, back_norm)
         x_rows(X_DA1, j, a1w).start()
 
-    send_y(U_UP)
+    z_relay(U_DOWN, 1)
+    z_relay(U_DOWN, 0)
 
     def ctx_back(s, carry):
         rows = rows_of(s)
@@ -790,42 +906,7 @@
         return carry
 
     lax.fori_loop(0, 4, attend_back, 0)
-
-    def input_back(i, carry):
-        s = lax.rem(i + 2, 4)
-        rows = rows_of(s)
-        value = contract(qkv[0, rows, :], w_qkv[0], 1, 1)
-        value = value + contract(qkv[1, rows, :], w_qkv[1], 1, 1)
-        value = value + contract(qkv[2, rows, :], w_qkv[2], 1, 1)
-        hand_over(X_DX, X_DH, s, value)
-        return carry
-
-    lax.fori_loop(0, 4, input_back, 0)
-
-    def grad_qkv(index, carry):
-        kind, i = index // 2, index % 2
-        value = contract(xw[:, span(i, 512)], qkv[kind], 0, 0).astype(BF)
-        for d in range(4):
-            for yy in range(2):
-                g_qkv[kind, d % 2, yy, i * 2 + d // 2] = (
-                    value[d * 128:(d + 1) * 128, yy * 256:(yy + 1) * 256]
-                )
-        return carry
-
-    def grad_out():
-        value = contract(ctx[...], a1w[...], 0, 0).astype(BF)
-        for d in range(8):
-            for yy in range(2):
-                g_out[d % 2, yy, d // 2] = value[yy * 256:(yy + 1) * 256, d * 128:(d + 1) * 128]
-
-    grad_out()
-    send_core(U_OUT)
-    for kind, u in ((0, U_Q), (1, U_K), (2, U_V)):
-        lax.fori_loop(kind * 2, kind * 2 + 2, grad_qkv, 0)
-        send_core(u)
-
-    def vec_piece(d):
-        return vg.at[d % 2, d // 2]
+    y_to_z(U_UP)
 
     for row in range(2, 8):
         line = jnp.sum(acc[row], axis=0, keepdims=True)
@@ -848,21 +929,59 @@
 
     def vec_z(k):
         to = lax.rem(z + k, ZS)
-        return remote(vg.at[c, to], vgz.at[k - 1], vs.at[2 + k], vr.at[2 + k], at_z[k - 1])
+        return remote(vg.at[c, to], vgz.at[k - 1], vs.at[2 + k], vr.at[2 + k], z_device(to))
 
     vec_x.start()
-    send_y(U_OUT)
-    send_z(U_DOWN)
-    send_y(U_Q)
+
+    def input_back(i, carry):
+        s = lax.rem(i + 2, 4)
+        rows = rows_of(s)
+        value = contract(qkv[0, rows, :], w_qkv[0], 1, 1)
+        value = value + contract(qkv[1, rows, :], w_qkv[1], 1, 1)
+        value = value + contract(qkv[2, rows, :], w_qkv[2], 1, 1)
+        hand_over(X_DX, X_DH, s, value)
+        return carry
+
+    lax.fori_loop(0, 2, input_back, 0)
     vec_x.wait()
     vg[...] = vg[...] + vgx[...]
     vec_c.start()
-    send_y(U_K)
-    send_y(U_V)
+
+    def grad_qkv(index, carry):
+        kind, i = index // 2, index % 2
+        value = contract(xw[:, span(i, 512)], qkv[kind], 0, 0).astype(BF)
+        for d in range(4):
+            for yy in range(2):
+                g_qkv[kind, d % 2, yy, i * 2 + d // 2] = (
+                    value[d * 128:(d + 1) * 128, yy * 256:(yy + 1) * 256]
+                )
+        return carry
+
+    def grad_out():
+        value = contract(ctx[...], a1w[...], 0, 0).astype(BF)
+        for d in range(8):
+            for yy in range(2):
+                g_out[d % 2, yy, d // 2] = value[yy * 256:(yy + 1) * 256, d * 128:(d + 1) * 128]
+
+    grad_out()
+    core_send(U_OUT)
+    for kind, u in ((0, U_Q), (1, U_K), (2, U_V)):
+        lax.fori_loop(kind * 2, kind * 2 + 2, grad_qkv, 0)
+        core_send(u)
     vec_c.wait()
     vg[c] = vg[c] + vgc[...]
     vec_y.start()
-    send_z(U_UP)
+    start(U_OUT)
+    start(U_Q)
+    start(U_K)
+    start(U_V)
+    lax.fori_loop(2, 4, input_back, 0)
+    z_relay(U_UP, 0)
+    vec_y.wait()
+    vg[c] = vg[c] + vgy[...]
+    for k in range(1, ZS):
+        vec_z(k).start()
+    y_to_z(U_OUT)
 
     def last_sum(j, other):
         x_sum(X_DX, j).wait_recv()
@@ -876,25 +995,23 @@
         tiles(j, body)
 
     last_sum(1 - y, True)
+    z_to_y(U_DOWN)
     go_on(remote(gts, gtr, ys.at[Y_GTOK], yr.at[Y_GTOK], at_y))
     last_sum(y, False)
     gtok_here = pltpu.make_async_copy(da.at[span(y, CHUNK)], gtok.at[y], os.at[7])
     gtok_here.start()
-    vec_y.wait()
-    vg[c] = vg[c] + vgy[...]
-    for k in range(1, ZS):
-        vec_z(k).start()
-    send_z(U_OUT)
-    send_z(U_Q)
-    send_z(U_K)
-    send_z(U_V)
-    finish(U_DOWN)
-    finish(U_UP)
+    z_relay(U_OUT, 0)
+    for u in (U_Q, U_K, U_V):
+        y_to_z(u)
+    for u in (U_Q, U_K, U_V):
+        z_relay(u, 0)
     for k in range(1, ZS):
         vec_z(k).wait()
     gvb[...] = vg[c, z] + vgz[0] + vgz[1] + vgz[2]
     vec_here = pltpu.make_async_copy(gvb.at[0:12], gv, os.at[8])
     vec_here.start()
+    finish(U_DOWN)
+    finish(U_UP)
     remote(gts, gtr, ys.at[Y_GTOK], yr.at[Y_GTOK], at_y).wait_recv()
     gtf[...] = gtr[...].astype(F32)
     gtok_there = pltpu.make_async_copy(gtf, gtok.at[1 - y], os.at[9])
@@ -911,6 +1028,12 @@
         x_sum(X_DX, j).wait_send()
     for copy in sent:
         copy.wait_send()
+    for condition, copy in later:
+        @pl.when(condition)
+        def _(copy=copy):
+            copy.wait_send()
+    for m in range(7):
+        remote(half_of(m), half_of(m), wsc.at[m], wrc.at[m], at_c).wait_send()
     for copy in finals + [out_here, gtok_here, gtok_there, vec_here]:
         copy.wait()
 
@@ -932,8 +1055,12 @@
         vmem((3, D, COLS), BF), vmem((COLS, D), BF), vmem((D, HID), BF), vmem((HID, D), BF),
         vmem((8, 12, 128), BF), vmem((16, D), F32),
     ]
-    for shape in ((2, 2, 4), (2, 4), (4,), (3,)):
-        scratch += [vmem(first + shape + piece, BF) for first, piece in zip(lead, pieces)]
+    ways = [2 if u in Z_FIRST else 1 for u in (U_DOWN, U_UP, U_OUT, U_Q)]
+    for shapes in (
+        [(2, 2, 4)] * 4, [(2, 4)] * 4, [(4,) if way == 1 else (1,) for way in ways],
+        [(way, 3) for way in ways], [(way,) for way in ways],
+    ):
+        scratch += [vmem(first + shape + piece, BF) for first, shape, piece in zip(lead, shapes, pieces)]
     scratch += [vmem((3, 128, 256), F32), vmem((256, 128), F32), vmem((128, 1024), F32), vmem((1024, 128), F32)]
     scratch += [
         vmem((SEQ, D), BF), vmem((3, SEQ, COLS), BF), vmem((SEQ, COLS), BF),
@@ -947,10 +1074,10 @@
         vmem((2, 4, 16, 128), F32), vmem((2, 4, 16, 128), F32), vmem((4, 16, 128), F32),
         vmem((4, 16, 128), F32), vmem((3, 16, 128), F32), vmem((16, 128), F32),
         vmem((SEQ, 128), F32), vmem((SEQ, 128), F32),
-        dma((5, 3)), dma((5, 3)), dma((4, 4)), dma((4, 4)), dma((5, 8)), dma((5, 8)),
+        dma((7, 2, 4)), dma((7, 2, 3)), dma((7, 4)), dma((7, 4)), dma((7,)), dma((7,)),
         dma((8, 2)), dma((8, 2)), dma((4,)), dma((4,)),
-        dma((6,)), dma((6,)), dma((6,)), dma((6,)), dma((6, 3)), dma((6, 3)),
-        dma((6,)), dma((6,)), dma((7,)), dma((10,)),
+        dma((6,)), dma((6,)), dma((6,)), dma((6,)), dma((6, 2, 4)), dma((6, 2, 4)),
+        dma((6,)), dma((6,)), dma((9,)), dma((10,)),
     ]
     hbm = pl.BlockSpec(memory_space=pl.ANY)
     return pl.pallas_call(

time: 246 us -> 207 us (0.84)
  the two profiles are of different devices: /device:TPU:25 before, /device:TPU:0 now
where the time goes in v2:
time: 207 us
  Pallas kernels  199 us (96%)
  local copies, waits for them, and re-layouts  7.47 us (4%)
    pallas_call x1, Pallas kernels, layer(): pl.pallas_call(layer_kernel, out_shape=outs, in_specs=[hbm, pl.BlockSpec(...  199 us
    unnamed x19, local copies, waits for them, and re-layouts  7.47 us

profile of v2, /device:TPU:0, one launch (start us, length us, event | category | flops | bytes accessed | tf_op | source)
XLA Modules:
  0.0 206.9 jit_solution(17354669428243345602)
XLA Ops:
  0.6 198.8 %shard_map.135 = (bf16[2,128,1024]{2,1,0:T(8,128)(2,1)}, f32[2,128,1024]{2,1,0:T(8,128)}, f32[3,128,256]{2,1,0:T(8,128)}, f32[256,128]{1,0:T(8,128)}, f32[128,10...) custom-call(bf16[2,128,1024]{2,1,0:T(8,128)(2,1)} %tok.1, s32[2,512]{1,0:T(2,128)} %seg.1, ...), custom_call_target="tpu_custom_call" | custom-call | tf_op jit(solution)/shard_map/pallas_call | solution.py:1083
  199.4 0.0 copy-start
  199.4 2.0 copy.22
  201.4 0.0 copy-done
  201.4 0.0 copy-start.3
  201.4 1.0 copy.23
  202.4 0.3 copy-done.3
  202.6 0.0 copy-start.4
  202.6 0.0 copy-start.2
  202.6 0.7 copy.24
  203.4 0.2 copy-done.4
  203.6 0.7 copy.25
  204.3 0.0 copy-done.2
  204.3 0.0 copy-start.1
  204.3 0.8 copy.26
  205.1 0.4 copy-done.1
  205.5 0.0 copy-start.5
  205.5 0.8 copy.27
  206.3 0.0 copy-done.5
  206.3 0.6 copy.28
Async XLA Ops:
  199.4 2.0 copy-start
  201.4 1.2 copy-start.3
  202.6 1.0 copy-start.4
  202.6 1.7 copy-start.2
  204.3 1.2 copy-start.1
  205.5 0.8 copy-start.5

commit v3 on v2

--- a/solution.py
+++ b/solution.py
@@ -265,10 +265,13 @@
 
 Y_TOK, Y_COT, Y_OUT, Y_GTOK = range(4)
 X_TOK, X_MIX, X_NORM, X_FFN, X_DA2, X_DH, X_DA1, X_DX = range(8)
-W_Q, W_K, W_V, W_OUT, W_UP, W_DOWN, W_VEC = range(7)
-Y_FIRST = (W_Q, W_OUT)
-Z_FIRST = (0,)
-U_DOWN, U_UP, U_OUT, U_V, U_K, U_Q = range(6)
+W_Q, W_K, W_V, W_OUT, W_UP, W_DOWN, W_REST, W_VEC = range(8)
+W_KINDS = 8
+Y_FIRST = (W_REST,)
+DIRECT = (W_VEC,)
+FAR_FIRST = ()
+U_DA, U_DB, U_UA, U_UB, U_OUT, U_V, U_K, U_Q = range(8)
+Z_FIRST = (U_DA, U_OUT)
 R_BQ, R_BV, R_BO, R_G1, R_C1, R_BD, R_G2, R_C2, R_BU = range(9)
 ZS = 4
 SEQ = 512
@@ -301,15 +304,15 @@
     w_qkv, w_out, w_up, w_down, w_vec, vf,
     g_down, g_up, g_out, g_qkv,
     c_down, c_up, c_out, c_qkv,
-    y_down, y_up, y_out, y_qkv,
-    z_down, z_up, z_out, z_qkv,
-    h_down, h_up, h_out, h_qkv,
+    y_da, y_db, y_up, y_out, y_qkv,
+    z_da, z_db, z_up, z_out, z_qkv,
+    h_da, h_db, h_up, h_out, h_qkv,
     o_qkv, o_out, o_up, o_down,
     xw, qkv, ctx, prob, bias, hw, act, slope, aw, a1w, dctx,
     own, n1, da, inv1, recv, stage, cotb, outb, gts, gtr, gtf,
     acc, vg, vgx, vgc, vgy, vgz, gvb, acc_k, acc_v,
-    wsz, wrz, wsy, wry, wsc, wrc, xs, xr, ys, yr,
-    gsc, grc, gsy, gry, gsz, grz, vs, vr, ls, os,
+    done, wrz, wry, wsc, wrc, wrd, fs, fr, xs, xr, yr,
+    grc, gry, grz, vs, vr, ls, os,
 ):
     dp = lax.axis_index("dp")
     tensor = lax.axis_index("tensor")
@@ -336,7 +339,7 @@
         copy.start()
         sent.append(copy)
 
-    args = [wq.at[0], wq.at[1], wq.at[2], wo, wu, wd, vec]
+    args = [wq.at[0], wq.at[1], wq.at[2], wo, wu, wd.at[0:512], wd.at[512:1024], vec]
     edge = jnp.logical_or(z == 0, z == ZS - 1)
     middle = jnp.logical_not(edge)
     later = []
@@ -357,8 +360,8 @@
             return w_out.at[span(yy, 256), span(d, 128)]
         if m == W_UP:
             return w_up.at[span(d, 128), span(yy, 1024)]
-        if m == W_DOWN:
-            return w_down.at[span(yy, 1024), span(d, 128)]
+        if m == W_DOWN or m == W_REST:
+            return w_down.at[span(yy * 2 + m - W_DOWN, 512), span(d, 128)]
         return w_vec.at[d]
 
     def from_z(k):
@@ -369,10 +372,11 @@
 
     def z_send(m, r):
         source = args[m] if r == 0 else place(m, 1 - y, dp)
-        for k, there in ((1, z != ZS - 1), (3, z != 0), (2, None)):
-            there = None if m == W_VEC else there
+        steps = ((1, z != ZS - 1), (3, z != 0), (2, None))
+        for k, there in (steps[2:] + steps[:2] if m in FAR_FIRST else steps):
+            there = None if m in DIRECT else there
             copy = remote(
-                source, place(m, column(r), dp), wsz.at[m, r, k - 1], wrz.at[m, r, k - 1],
+                source, place(m, column(r), dp), done.at[0], wrz.at[m, r, k - 1],
                 z_device(lax.rem(z + k, ZS)),
             )
             if there is None:
@@ -380,40 +384,92 @@
             else:
                 go_if(there, copy)
 
-    def z_serve(m, r, step):
+    def z_serve(m, r, step, keep=False):
+        z_take(m, r, step, keep)
+        z_note(m, r, step)
+
+    def z_serve_split(m, r, step, early, late):
+        def first():
+            @pl.when(early)
+            def _():
+                z_take(m, r, step)
+
+        def second():
+            @pl.when(late)
+            def _():
+                z_take(m, r, step)
+            z_note(m, r, step)
+        return first, second
+
+    def z_parts(m, r, step):
         k = (jnp.where(z == 0, 3, 1), 2, jnp.where(z == 0, 1, 3))[step]
         here = place(m, column(r), from_z(k) * 2 + c)
-        remote(here, here, wsz.at[m, r, k - 1], wrz.at[m, r, k - 1], at_x).wait_recv()
-        if step == 1 and m != W_VEC:
-            slot = jnp.where(z == 1, 0, 2)
-            go_if(middle, remote(
-                here, here, wsz.at[m, r, 3], wrz.at[m, r, slot], z_device(jnp.where(z == 1, 0, 3)),
-            ))
+        slot = jnp.where(z == 1, 0, 2)
+        hand_on = None
+        if step == 1 and m not in DIRECT:
+            hand_on = remote(
+                here, here, done.at[0], wrz.at[m, r, slot], z_device(jnp.where(z == 1, 0, 3)),
+            )
+        over_y = None
         if r == 0 and m not in Y_FIRST and m != W_VEC:
-            go_on(remote(here, here, wsy.at[m, k], wry.at[m, from_z(k)], at_y))
-        c_send(m, here)
+            over_y = remote(here, here, done.at[0], wry.at[m, from_z(k)], at_y)
+        return k, here, hand_on, over_y
+
+    def z_over(m, step):
+        z_parts(m, 0, step)[3].start()
+
+    def z_take(m, r, step, keep=False):
+        k, here, hand_on, over_y = z_parts(m, r, step)
+        remote(here, here, done.at[0], wrz.at[m, r, k - 1], at_x).wait_recv()
+        if hand_on is not None:
+            @pl.when(middle)
+            def _():
+                hand_on.start()
+        if over_y is not None and not keep:
+            over_y.start()
+        c_send(m, here, step + 1)
+
+    def z_note(m, r, step):
+        _, _, hand_on, over_y = z_parts(m, r, step)
+        if hand_on is not None:
+            later.append((middle, hand_on))
+        if over_y is not None:
+            sent.append(over_y)
 
     def y_send(m):
-        go_on(remote(args[m], place(m, y, dp), wsy.at[m, 0], wry.at[m, z], at_y))
+        go_on(remote(args[m], place(m, y, dp), done.at[0], wry.at[m, z], at_y))
+
+    def source_of(step):
+        return z if step == 0 else from_z((jnp.where(z == 0, 3, 1), 2, jnp.where(z == 0, 1, 3))[step - 1])
 
     def y_serve(m, step):
-        zz = lax.rem(z + step, ZS)
+        zz = source_of(step)
         here = place(m, 1 - y, zz * 2 + c)
-        remote(here, here, wsy.at[m, 0], wry.at[m, zz], at_y).wait_recv()
-        c_send(m, here)
-
-    def c_send(m, source, dest=None):
+        remote(here, here, done.at[0], wry.at[m, zz], at_y).wait_recv()
+        c_send(m, here, step)
+
+    def c_send(m, source, step, dest=None):
         dest = source if dest is None else dest
-        remote(source, dest, wsc.at[m], wrc.at[m], at_c).start()
+        into = wrd.at[m - W_DOWN, step] if m in (W_DOWN, W_REST) else wrc.at[m]
+        remote(source, dest, wsc.at[m], into, at_c).start()
 
     def own_send(m):
-        c_send(m, args[m], place(m, y, dp))
+        c_send(m, args[m], 0, place(m, y, dp))
         pltpu.make_async_copy(args[m], place(m, y, dp), ls.at[m]).start()
 
     def half_of(m):
         if m <= W_V:
             return w_qkv.at[m, :, 0:256]
-        return (w_out.at[0:256], w_up.at[:, 0:1024], w_down.at[0:1024], w_vec.at[0:4])[m - W_OUT]
+        return (
+            w_out.at[0:256], w_up.at[:, 0:1024], w_down.at[0:512], w_down.at[0:512], w_vec.at[0:4]
+        )[m - W_OUT]
+
+    def wait_down(step):
+        for m in (W_DOWN, W_REST):
+            if step == 0:
+                pltpu.make_async_copy(args[m], place(m, y, dp), ls.at[m]).wait()
+            two = w_down.at[0:1024, 0:128]
+            remote(two, two, wsc.at[m], wrd.at[m - W_DOWN, step], at_c).wait_recv()
 
     def wait_weight(m):
         pltpu.make_async_copy(args[m], place(m, y, dp), ls.at[m]).wait()
@@ -428,15 +484,14 @@
     for m in (W_Q, W_K, W_V):
         y_send(m)
         z_send(m, 0)
-    y_send(W_OUT)
-    go_on(remote(tok.at[1 - y], xw.at[tok_rows(x, y)], ys.at[Y_TOK], yr.at[Y_TOK], at_y))
+    go_on(remote(tok.at[1 - y], xw.at[tok_rows(x, y)], done.at[0], yr.at[Y_TOK], at_y))
     go_on(x_copy(X_TOK, 0, tok.at[y], xw.at[tok_rows(x, y)]))
     z_send(W_VEC, 0)
-    for m in range(7):
+    for m in range(W_KINDS):
         own_send(m)
-    local_x = pltpu.make_async_copy(tok.at[y], xw.at[tok_rows(x, y)], ls.at[7])
+    local_x = pltpu.make_async_copy(tok.at[y], xw.at[tok_rows(x, y)], ls.at[8])
     local_x.start()
-    local_cot = pltpu.make_async_copy(cot.at[y], cotb.at[span(y, CHUNK)], ls.at[8])
+    local_cot = pltpu.make_async_copy(cot.at[y], cotb.at[span(y, CHUNK)], ls.at[9])
     local_cot.start()
 
     seg_row = seg[pl.ds(y, 1), :].astype(F32)
@@ -451,32 +506,27 @@
     acc[...] = jnp.zeros_like(acc)
     vg[...] = jnp.zeros_like(vg)
 
-    y_serve(W_Q, 0)
-    z_send(W_Q, 1)
-    y_serve(W_OUT, 0)
     for step in range(2):
-        for m in (W_K, W_V, W_Q):
+        for m in (W_Q, W_K, W_V):
             z_serve(m, 0, step)
     z_send(W_OUT, 0)
-    z_send(W_OUT, 1)
     y_tok_here = xw.at[tok_rows(x, 1 - y)]
-    remote(tok.at[1 - y], y_tok_here, ys.at[Y_TOK], yr.at[Y_TOK], at_y).wait_recv()
+    remote(tok.at[1 - y], y_tok_here, done.at[0], yr.at[Y_TOK], at_y).wait_recv()
     go_on(x_copy(X_TOK, 1, y_tok_here, y_tok_here))
-    z_serve(W_Q, 1, 0)
-    z_serve(W_Q, 1, 1)
-    for m in (W_K, W_V, W_Q):
+    for m in (W_Q, W_K, W_V):
         z_serve(m, 0, 2)
-    z_serve(W_Q, 1, 2)
+    y_send(W_OUT)
+    z_serve(W_OUT, 0, 0)
+    z_serve(W_OUT, 0, 1)
     z_send(W_UP, 0)
-    y_send(W_UP)
-    for r in range(2):
-        for step in range(2):
-            z_serve(W_OUT, r, step)
     for step in range(3):
         z_serve(W_VEC, 0, step)
+    z_serve(W_OUT, 0, 2)
+    y_send(W_UP)
+    y_send(W_REST)
     for step in range(4):
-        y_serve(W_K, step)
-        y_serve(W_V, step)
+        for m in (W_Q, W_K, W_V):
+            y_serve(m, step)
     wait_weight(W_VEC)
     for d in range(8):
         vf[0:12, d * 128:(d + 1) * 128] = w_vec[d].astype(F32)
@@ -528,13 +578,12 @@
 
     z_serve(W_UP, 0, 0)
     lax.fori_loop(0, 4, attend, 0)
-    z_serve(W_UP, 0, 1)
+    for step in range(4):
+        y_serve(W_OUT, step)
+    lax.fori_loop(4, 8, attend, 0)
+    up_early, up_late = z_serve_split(W_UP, 0, 1, middle, edge)
+    up_early()
     z_send(W_DOWN, 0)
-    z_serve(W_OUT, 0, 2)
-    z_serve(W_OUT, 1, 2)
-    lax.fori_loop(4, 8, attend, 0)
-    z_serve(W_UP, 0, 2)
-    y_send(W_DOWN)
 
     def rows_of(s):
         mine = jnp.where(s < 2, x, 1 - x)
@@ -567,9 +616,14 @@
         return carry
 
     lax.fori_loop(0, 4, mix, 0)
-    z_serve(W_DOWN, 0, 0)
+    up_late()
+    z_serve(W_UP, 0, 2)
+    y_serve(W_REST, 0)
+    z_send(W_REST, 0)
+    z_send(W_REST, 1)
     y_serve(W_UP, 0)
-    y_serve(W_UP, 1)
+    z_serve(W_DOWN, 0, 0, keep=True)
+    z_serve(W_DOWN, 0, 1, keep=True)
 
     def row_of(row):
         return vf[row:row + 1, :]
@@ -603,9 +657,15 @@
         tiles(j, first_norm)
         x_rows(X_NORM, j, hw).start()
 
-    z_serve(W_DOWN, 0, 1)
-    y_serve(W_UP, 2)
-    y_serve(W_UP, 3)
+    y_send(W_DOWN)
+    z_over(W_DOWN, 0)
+    z_over(W_DOWN, 1)
+    for step in range(1, 4):
+        y_serve(W_UP, step)
+    z_serve(W_DOWN, 0, 2)
+    for r in range(2):
+        z_serve(W_REST, r, 0)
+        z_serve(W_REST, r, 1)
     wait_weight(W_UP)
 
     def arrived(kind, s, buf):
@@ -630,19 +690,28 @@
         return carry
 
     lax.fori_loop(0, 2, ffn_up, 0)
-    z_serve(W_DOWN, 0, 2)
-    lax.fori_loop(2, 4, ffn_up, 0)
-    go_on(remote(cot.at[1 - y], cotb.at[span(y, CHUNK)], ys.at[Y_COT], yr.at[Y_COT], at_y))
+    y_serve(W_DOWN, 0)
+    y_serve(W_DOWN, 1)
+    lax.fori_loop(2, 3, ffn_up, 0)
+    z_serve(W_REST, 0, 2)
+    z_serve(W_REST, 1, 2)
+    y_serve(W_DOWN, 2)
+    lax.fori_loop(3, 4, ffn_up, 0)
+    y_serve(W_DOWN, 3)
+    go_on(remote(cot.at[1 - y], cotb.at[span(y, CHUNK)], done.at[0], yr.at[Y_COT], at_y))
+
+    def ffn_copy(step):
+        cols = span(source_of(step), 256)
+        return remote(stage.at[:, cols], recv.at[:, cols], fs.at[step], fr.at[step], at_x)
+
+    for j in range(2):
+        x_sum(X_MIX, j).wait_send()
     for step in range(4):
-        y_serve(W_DOWN, step)
-    wait_weight(W_DOWN)
-
-    def ffn_down(i, carry):
-        s = lax.rem(i + 2, 4)
-        hand_over(X_FFN, X_MIX, s, contract(act[rows_of(s), :], w_down[...], 1, 0))
-        return carry
-
-    lax.fori_loop(0, 4, ffn_down, 0)
+        wait_down(step)
+        cols = span(source_of(step), 256)
+        stage[:, cols] = contract(act[span(1 - x, ROWS), :], w_down[:, cols], 1, 0).astype(BF)
+        ffn_copy(step).start()
+        own[:, cols] = contract(act[span(x, ROWS), :], w_down[:, cols], 1, 0)
 
     def bump(row, value):
         acc[row] += fold_rows(value)
@@ -661,14 +730,15 @@
 
     local_cot.wait()
     cot_here = cotb.at[span(1 - y, CHUNK)]
-    remote(cot.at[1 - y], cot_here, ys.at[Y_COT], yr.at[Y_COT], at_y).wait_recv()
+    remote(cot.at[1 - y], cot_here, done.at[0], yr.at[Y_COT], at_y).wait_recv()
+    for step in range(4):
+        ffn_copy(step).wait()
     for j in range(2):
-        x_sum(X_FFN, j).wait_recv()
         tiles(j, second_norm)
         x_rows(X_DA2, j, aw).start()
     out_here = pltpu.make_async_copy(outb.at[span(y, CHUNK)], out.at[y], os.at[0])
     out_here.start()
-    go_on(remote(outb.at[span(1 - y, CHUNK)], out.at[y], ys.at[Y_OUT], yr.at[Y_OUT], at_y))
+    go_on(remote(outb.at[span(1 - y, CHUNK)], out.at[y], done.at[0], yr.at[Y_OUT], at_y))
 
     def ffn_back(s, carry):
         rows = rows_of(s)
@@ -678,16 +748,19 @@
             grad = contract(aw[rows, :], w_down[cols, :], 1, 1) * slope[rows, cols].astype(F32)
             bump(R_BU + n, grad)
             slope[rows, cols] = grad.astype(BF)
-        hand_over(X_DH, X_FFN, s, contract(slope[rows, :], w_up[...], 1, 1))
+        hand_over(X_DH, None, s, contract(slope[rows, :], w_up[...], 1, 1))
         return carry
 
     lax.fori_loop(0, 4, ffn_back, 0)
 
     units = {
-        U_DOWN: (g_down, c_down, y_down, z_down, h_down, o_down, gd),
-        U_UP: (g_up, c_up, y_up, z_up, h_up, o_up, gu),
+        U_DA: (g_down.at[0], c_down.at[0], y_da, z_da, h_da, o_down.at[0:512], gd.at[0:512]),
+        U_DB: (g_down.at[1], c_down.at[1], y_db, z_db, h_db, o_down.at[512:1024], gd.at[512:1024]),
         U_OUT: (g_out, c_out, y_out, z_out, h_out, o_out, go),
     }
+    for u, i in ((U_UA, 0), (U_UB, 1)):
+        rows = slice(i * 64, (i + 1) * 64)
+        units[u] = tuple(r.at[i] for r in (g_up, c_up, y_up, z_up, h_up)) + (o_up.at[rows], gu.at[rows])
     for u, i in ((U_Q, 0), (U_K, 1), (U_V, 2)):
         units[u] = tuple(r.at[i] for r in (g_qkv, c_qkv, y_qkv, z_qkv, h_qkv, o_qkv, gq))
 
@@ -706,7 +779,7 @@
 
     def core_copy(u):
         g, rc = units[u][0], units[u][1]
-        return remote(g.at[1 - c], rc, gsc.at[u], grc.at[u], at_c)
+        return remote(g.at[1 - c], rc, done.at[0], grc.at[u], at_c)
 
     def core_send(u):
         go_on(core_copy(u))
@@ -719,17 +792,17 @@
     def rs_y_copy(u):
         g, ry = units[u][0], units[u][2]
         source = g.at[c, 1 - y, pl.ds(z, 1)] if u in Z_FIRST else g.at[c, 1 - y]
-        return remote(source, ry, gsy.at[u], gry.at[u], at_y)
+        return remote(source, ry, done.at[0], gry.at[u], at_y)
 
     def rs_z_copy(u, r, k):
         g, rz = units[u][0], units[u][3]
         to = lax.rem(z + k, ZS)
-        return remote(g.at[c, column(r), to], rz.at[r, k - 1], gsz.at[u, r, k - 1], grz.at[u, r, k - 1], z_device(to))
+        return remote(g.at[c, column(r), to], rz.at[r, k - 1], done.at[0], grz.at[u, r, k - 1], z_device(to))
 
     def rs_hand_on(u, r):
         g, rh = units[u][0], units[u][4]
         far = jnp.where(z == 0, ZS - 1, 0)
-        return remote(g.at[c, column(r), far], rh.at[r], gsz.at[u, r, 3], grz.at[u, r, 3], z_device(jnp.where(z == 0, 1, 2)))
+        return remote(g.at[c, column(r), far], rh.at[r], done.at[0], grz.at[u, r, 3], z_device(jnp.where(z == 0, 1, 2)))
 
     def z_hand_on(u, r):
         go_if(edge, rs_hand_on(u, r))
@@ -823,25 +896,32 @@
                     rz[r, k - 1] = jnp.zeros(rz.shape[2:], BF)
 
     def grad_down(i, carry):
-        value = contract(act[:, span(i, 512)], aw[...], 0, 0).astype(BF)
+        half, yy = 1 - i // 2, i % 2
+        value = contract(act[:, span(yy * 2 + half, 512)], aw[...], 0, 0).astype(BF)
         for d in range(8):
-            g_down[d % 2, i // 2, d // 2, span(i % 2, 512), :] = value[:, d * 128:(d + 1) * 128]
+            g_down[half, d % 2, yy, d // 2] = value[:, d * 128:(d + 1) * 128]
         return carry
 
-    lax.fori_loop(0, 4, grad_down, 0)
-    core_send(U_DOWN)
+    lax.fori_loop(0, 2, grad_down, 0)
+    core_send(U_DB)
+    lax.fori_loop(2, 4, grad_down, 0)
+    core_send(U_DA)
+    start(U_DB)
 
     def grad_up(index, carry):
         i, n = index // 2, index % 2
         value = contract(hw[:, span(i, 512)], slope[:, span(n, 1024)], 0, 0).astype(BF)
         for d in range(4):
-            g_up[d % 2, n, i * 2 + d // 2] = value[d * 128:(d + 1) * 128, :]
+            for part in range(2):
+                r = d * 128 + part * 64
+                g_up[part, d % 2, n, i * 2 + d // 2] = value[r:r + 64, :]
         return carry
 
     lax.fori_loop(0, 4, grad_up, 0)
-    core_send(U_UP)
-    start(U_DOWN)
-    start(U_UP)
+    core_send(U_UA)
+    core_send(U_UB)
+    for u in (U_DA, U_UA, U_UB):
+        start(u)
 
     def back_norm(r, g):
         grad = da[r, :] + own[r, :] + recv[r, :].astype(F32)
@@ -858,8 +938,8 @@
         tiles(j, back_norm)
         x_rows(X_DA1, j, a1w).start()
 
-    z_relay(U_DOWN, 1)
-    z_relay(U_DOWN, 0)
+    z_relay(U_DA, 1)
+    z_relay(U_DA, 0)
 
     def ctx_back(s, carry):
         rows = rows_of(s)
@@ -905,8 +985,16 @@
                     qkv[i, 128:SEQ, lanes] = (total[128:SEQ, :] + more).astype(BF)
         return carry
 
+    def grad_out():
+        value = contract(ctx[...], a1w[...], 0, 0).astype(BF)
+        for d in range(8):
+            for yy in range(2):
+                g_out[d % 2, yy, d // 2] = value[yy * 256:(yy + 1) * 256, d * 128:(d + 1) * 128]
+
+    grad_out()
+    core_send(U_OUT)
+    y_to_z(U_DB)
     lax.fori_loop(0, 4, attend_back, 0)
-    y_to_z(U_UP)
 
     for row in range(2, 8):
         line = jnp.sum(acc[row], axis=0, keepdims=True)
@@ -943,6 +1031,9 @@
         return carry
 
     lax.fori_loop(0, 2, input_back, 0)
+    start(U_OUT)
+    z_relay(U_DB, 0)
+    y_to_z(U_UA)
     vec_x.wait()
     vg[...] = vg[...] + vgx[...]
     vec_c.start()
@@ -957,31 +1048,22 @@
                 )
         return carry
 
-    def grad_out():
-        value = contract(ctx[...], a1w[...], 0, 0).astype(BF)
-        for d in range(8):
-            for yy in range(2):
-                g_out[d % 2, yy, d // 2] = value[yy * 256:(yy + 1) * 256, d * 128:(d + 1) * 128]
-
-    grad_out()
-    core_send(U_OUT)
     for kind, u in ((0, U_Q), (1, U_K), (2, U_V)):
         lax.fori_loop(kind * 2, kind * 2 + 2, grad_qkv, 0)
         core_send(u)
     vec_c.wait()
     vg[c] = vg[c] + vgc[...]
     vec_y.start()
-    start(U_OUT)
-    start(U_Q)
-    start(U_K)
-    start(U_V)
+    for u in (U_Q, U_K, U_V):
+        start(u)
+    y_to_z(U_UB)
     lax.fori_loop(2, 4, input_back, 0)
-    z_relay(U_UP, 0)
+    z_relay(U_OUT, 1)
+    z_relay(U_OUT, 0)
     vec_y.wait()
     vg[c] = vg[c] + vgy[...]
     for k in range(1, ZS):
         vec_z(k).start()
-    y_to_z(U_OUT)
 
     def last_sum(j, other):
         x_sum(X_DX, j).wait_recv()
@@ -995,32 +1077,35 @@
         tiles(j, body)
 
     last_sum(1 - y, True)
-    z_to_y(U_DOWN)
-    go_on(remote(gts, gtr, ys.at[Y_GTOK], yr.at[Y_GTOK], at_y))
+    go_on(remote(gts, gtr, done.at[0], yr.at[Y_GTOK], at_y))
     last_sum(y, False)
-    gtok_here = pltpu.make_async_copy(da.at[span(y, CHUNK)], gtok.at[y], os.at[7])
+    gtok_here = pltpu.make_async_copy(da.at[span(y, CHUNK)], gtok.at[y], os.at[9])
     gtok_here.start()
-    z_relay(U_OUT, 0)
-    for u in (U_Q, U_K, U_V):
-        y_to_z(u)
+    z_relay(U_UA, 0)
+    y_to_z(U_Q)
+    z_to_y(U_DA)
+    y_to_z(U_K)
+    z_relay(U_UB, 0)
+    z_to_y(U_OUT)
+    y_to_z(U_V)
     for u in (U_Q, U_K, U_V):
         z_relay(u, 0)
     for k in range(1, ZS):
         vec_z(k).wait()
     gvb[...] = vg[c, z] + vgz[0] + vgz[1] + vgz[2]
-    vec_here = pltpu.make_async_copy(gvb.at[0:12], gv, os.at[8])
+    vec_here = pltpu.make_async_copy(gvb.at[0:12], gv, os.at[10])
     vec_here.start()
-    finish(U_DOWN)
-    finish(U_UP)
-    remote(gts, gtr, ys.at[Y_GTOK], yr.at[Y_GTOK], at_y).wait_recv()
+    for u in (U_DA, U_DB, U_UA, U_UB):
+        finish(u)
+    remote(gts, gtr, done.at[0], yr.at[Y_GTOK], at_y).wait_recv()
     gtf[...] = gtr[...].astype(F32)
-    gtok_there = pltpu.make_async_copy(gtf, gtok.at[1 - y], os.at[9])
+    gtok_there = pltpu.make_async_copy(gtf, gtok.at[1 - y], os.at[11])
     gtok_there.start()
     finish(U_OUT)
     finish(U_Q)
     finish(U_K)
     finish(U_V)
-    remote(outb.at[span(1 - y, CHUNK)], out.at[1 - y], ys.at[Y_OUT], yr.at[Y_OUT], at_y).wait_recv()
+    remote(outb.at[span(1 - y, CHUNK)], out.at[1 - y], done.at[0], yr.at[Y_OUT], at_y).wait_recv()
     for kind, buf in ((X_NORM, hw), (X_DA2, aw), (X_DA1, a1w)):
         for j in range(2):
             x_rows(kind, j, buf).wait_send()
@@ -1032,7 +1117,7 @@
         @pl.when(condition)
         def _(copy=copy):
             copy.wait_send()
-    for m in range(7):
+    for m in range(W_KINDS):
         remote(half_of(m), half_of(m), wsc.at[m], wrc.at[m], at_c).wait_send()
     for copy in finals + [out_here, gtok_here, gtok_there, vec_here]:
         copy.wait()
@@ -1049,18 +1134,22 @@
         jax.ShapeDtypeStruct(w_down.shape, F32),
         jax.ShapeDtypeStruct(vectors.shape, F32),
     )
-    pieces = ((1024, 128), (128, 1024), (256, 128), (128, 256))
-    lead = ((), (), (), (3,))
     scratch = [
         vmem((3, D, COLS), BF), vmem((COLS, D), BF), vmem((D, HID), BF), vmem((HID, D), BF),
         vmem((8, 12, 128), BF), vmem((16, D), F32),
     ]
-    ways = [2 if u in Z_FIRST else 1 for u in (U_DOWN, U_UP, U_OUT, U_Q)]
-    for shapes in (
-        [(2, 2, 4)] * 4, [(2, 4)] * 4, [(4,) if way == 1 else (1,) for way in ways],
-        [(way, 3) for way in ways], [(way,) for way in ways],
-    ):
-        scratch += [vmem(first + shape + piece, BF) for first, shape, piece in zip(lead, shapes, pieces)]
+    half_down, half_up, piece_out, piece_qkv = (512, 128), (64, 1024), (256, 128), (128, 256)
+    for shape in ((2, 2, 4), (2, 4)):
+        scratch += [
+            vmem((2,) + shape + half_down, BF), vmem((2,) + shape + half_up, BF),
+            vmem(shape + piece_out, BF), vmem((3,) + shape + piece_qkv, BF),
+        ]
+    for y_shape, z_shape in (((4,), (1,)), ((1, 3), (2, 3)), ((1,), (2,))):
+        scratch += [
+            vmem(z_shape + half_down, BF), vmem(y_shape + half_down, BF),
+            vmem((2,) + y_shape + half_up, BF), vmem(z_shape + piece_out, BF),
+            vmem((3,) + y_shape + piece_qkv, BF),
+        ]
     scratch += [vmem((3, 128, 256), F32), vmem((256, 128), F32), vmem((128, 1024), F32), vmem((1024, 128), F32)]
     scratch += [
         vmem((SEQ, D), BF), vmem((3, SEQ, COLS), BF), vmem((SEQ, COLS), BF),
@@ -1074,10 +1163,10 @@
         vmem((2, 4, 16, 128), F32), vmem((2, 4, 16, 128), F32), vmem((4, 16, 128), F32),
         vmem((4, 16, 128), F32), vmem((3, 16, 128), F32), vmem((16, 128), F32),
         vmem((SEQ, 128), F32), vmem((SEQ, 128), F32),
-        dma((7, 2, 4)), dma((7, 2, 3)), dma((7, 4)), dma((7, 4)), dma((7,)), dma((7,)),
-        dma((8, 2)), dma((8, 2)), dma((4,)), dma((4,)),
-        dma((6,)), dma((6,)), dma((6,)), dma((6,)), dma((6, 2, 4)), dma((6, 2, 4)),
-        dma((6,)), dma((6,)), dma((9,)), dma((10,)),
+        dma((1,)), dma((8, 2, 3)), dma((8, 4)), dma((8,)), dma((8,)), dma((2, 4)), dma((4,)), dma((4,)),
+        dma((8, 2)), dma((8, 2)), dma((4,)),
+        dma((8,)), dma((8,)), dma((8, 2, 4)),
+        dma((6,)), dma((6,)), dma((10,)), dma((12,)),
     ]
     hbm = pl.BlockSpec(memory_space=pl.ANY)
     return pl.pallas_call(

time: 207 us -> 193 us (0.932)
  Pallas kernels: 199 us -> 185 us
    pallas_call x1, Pallas kernels: 199 us -> 185 us  [layer(): pl.pallas_call(layer_kernel, out_shape=outs, in_specs=[hbm, pl.BlockSpec(...]
where the time goes in v3:
time: 193 us
  Pallas kernels  185 us (96%)
  local copies, waits for them, and re-layouts  7.47 us (4%)
    pallas_call x1, Pallas kernels, layer(): pl.pallas_call(layer_kernel, out_shape=outs, in_specs=[hbm, pl.BlockSpec(...  185 us
    unnamed x19, local copies, waits for them, and re-layouts  7.47 us

profile of v3, /device:TPU:0, one launch (start us, length us, event | category | flops | bytes accessed | tf_op | source)
XLA Modules:
  0.0 192.9 jit_solution(4593136614129105153)
XLA Ops:
  0.6 184.7 %shard_map.135 = (bf16[2,128,1024]{2,1,0:T(8,128)(2,1)}, f32[2,128,1024]{2,1,0:T(8,128)}, f32[3,128,256]{2,1,0:T(8,128)}, f32[256,128]{1,0:T(8,128)}, f32[128,10...) custom-call(bf16[2,128,1024]{2,1,0:T(8,128)(2,1)} %tok.1, s32[2,512]{1,0:T(2,128)} %seg.1, ...), custom_call_target="tpu_custom_call" | custom-call | tf_op jit(solution)/shard_map/pallas_call | solution.py:1172
  185.4 0.0 copy-start
  185.4 2.0 %copy.22 = bf16[2,128,1024]{2,1,0:T(8,128)(2,1)} copy(bf16[2,128,1024]{2,1,0:T(8,128)(2,1)} %get-tuple-element.14) | data formatting | bytes 1048576
  187.3 0.0 copy-done
  187.3 0.0 copy-start.3
  187.3 1.0 copy.23
  188.3 0.3 copy-done.3
  188.6 0.0 copy-start.4
  188.6 0.0 copy-start.2
  188.6 0.7 copy.24
  189.3 0.2 copy-done.4
  189.6 0.7 copy.25
  190.2 0.0 copy-done.2
  190.2 0.0 copy-start.1
  190.2 0.8 copy.26
  191.0 0.4 copy-done.1
  191.5 0.0 copy-start.5
  191.5 0.8 copy.27
  192.3 0.0 copy-done.5
  192.3 0.6 copy.28
Async XLA Ops:
  185.4 2.0 %copy-start = (f32[2,128,1024]{2,1,0:T(8,128)S(1)}, f32[2,128,1024]{2,1,0:T(8,128)}, u32[]{:S(2)}) copy-start(f32[2,128,1024]{2,1,0:T(8,128)} %get-tuple-element.15) | copy-start | bytes 3145732
  187.3 1.2 copy-start.3
  188.6 1.0 copy-start.4
  188.6 1.7 copy-start.2
  190.2 1.2 copy-start.1
  191.5 0.8 copy-start.5

commit v4 on v3

--- a/solution.py
+++ b/solution.py
@@ -311,7 +311,7 @@
     xw, qkv, ctx, prob, bias, hw, act, slope, aw, a1w, dctx,
     own, n1, da, inv1, recv, stage, cotb, outb, gts, gtr, gtf,
     acc, vg, vgx, vgc, vgy, vgz, gvb, acc_k, acc_v,
-    done, wrz, wry, wsc, wrc, wrd, fs, fr, xs, xr, yr,
+    done, wrz, wry, wrc, wrd, fs, fr, xs, xr, yr,
     grc, gry, grz, vs, vr, ls, os,
 ):
     dp = lax.axis_index("dp")
@@ -363,6 +363,9 @@
         if m == W_DOWN or m == W_REST:
             return w_down.at[span(yy * 2 + m - W_DOWN, 512), span(d, 128)]
         return w_vec.at[d]
+
+    even = lax.rem(z, 2) == 0
+    near_first = (jnp.where(even, 3, 1), 2, jnp.where(even, 1, 3))
 
     def from_z(k):
         return lax.rem(z + ZS - k, ZS)
@@ -402,7 +405,7 @@
         return first, second
 
     def z_parts(m, r, step):
-        k = (jnp.where(z == 0, 3, 1), 2, jnp.where(z == 0, 1, 3))[step]
+        k = near_first[step]
         here = place(m, column(r), from_z(k) * 2 + c)
         slot = jnp.where(z == 1, 0, 2)
         hand_on = None
@@ -440,7 +443,7 @@
         go_on(remote(args[m], place(m, y, dp), done.at[0], wry.at[m, z], at_y))
 
     def source_of(step):
-        return z if step == 0 else from_z((jnp.where(z == 0, 3, 1), 2, jnp.where(z == 0, 1, 3))[step - 1])
+        return z if step == 0 else from_z(near_first[step - 1])
 
     def y_serve(m, step):
         zz = source_of(step)
@@ -451,7 +454,7 @@
     def c_send(m, source, step, dest=None):
         dest = source if dest is None else dest
         into = wrd.at[m - W_DOWN, step] if m in (W_DOWN, W_REST) else wrc.at[m]
-        remote(source, dest, wsc.at[m], into, at_c).start()
+        remote(source, dest, done.at[0], into, at_c).start()
 
     def own_send(m):
         c_send(m, args[m], 0, place(m, y, dp))
@@ -469,11 +472,11 @@
             if step == 0:
                 pltpu.make_async_copy(args[m], place(m, y, dp), ls.at[m]).wait()
             two = w_down.at[0:1024, 0:128]
-            remote(two, two, wsc.at[m], wrd.at[m - W_DOWN, step], at_c).wait_recv()
+            remote(two, two, done.at[0], wrd.at[m - W_DOWN, step], at_c).wait_recv()
 
     def wait_weight(m):
         pltpu.make_async_copy(args[m], place(m, y, dp), ls.at[m]).wait()
-        remote(half_of(m), half_of(m), wsc.at[m], wrc.at[m], at_c).wait_recv()
+        remote(half_of(m), half_of(m), done.at[0], wrc.at[m], at_c).wait_recv()
 
     def x_copy(kind, j, src, dst):
         return remote(src, dst, xs.at[kind, j], xr.at[kind, j], at_x)
@@ -662,10 +665,6 @@
     z_over(W_DOWN, 1)
     for step in range(1, 4):
         y_serve(W_UP, step)
-    z_serve(W_DOWN, 0, 2)
-    for r in range(2):
-        z_serve(W_REST, r, 0)
-        z_serve(W_REST, r, 1)
     wait_weight(W_UP)
 
     def arrived(kind, s, buf):
@@ -690,27 +689,38 @@
         return carry
 
     lax.fori_loop(0, 2, ffn_up, 0)
+    z_serve(W_DOWN, 0, 2)
+    for r in range(2):
+        z_serve(W_REST, r, 0)
+        z_serve(W_REST, r, 1)
     y_serve(W_DOWN, 0)
+    lax.fori_loop(2, 3, ffn_up, 0)
     y_serve(W_DOWN, 1)
-    lax.fori_loop(2, 3, ffn_up, 0)
+    lax.fori_loop(3, 4, ffn_up, 0)
+    y_serve(W_DOWN, 2)
     z_serve(W_REST, 0, 2)
     z_serve(W_REST, 1, 2)
-    y_serve(W_DOWN, 2)
-    lax.fori_loop(3, 4, ffn_up, 0)
-    y_serve(W_DOWN, 3)
     go_on(remote(cot.at[1 - y], cotb.at[span(y, CHUNK)], done.at[0], yr.at[Y_COT], at_y))
 
-    def ffn_copy(step):
+    def ffn_copy(step, j):
         cols = span(source_of(step), 256)
-        return remote(stage.at[:, cols], recv.at[:, cols], fs.at[step], fr.at[step], at_x)
+        return remote(
+            stage.at[span(j, CHUNK), cols], recv.at[span(j, CHUNK), cols],
+            fs.at[step, j], fr.at[step, j], at_x,
+        )
 
     for j in range(2):
         x_sum(X_MIX, j).wait_send()
     for step in range(4):
+        if step == 2:
+            y_serve(W_DOWN, 3)
         wait_down(step)
         cols = span(source_of(step), 256)
         stage[:, cols] = contract(act[span(1 - x, ROWS), :], w_down[:, cols], 1, 0).astype(BF)
-        ffn_copy(step).start()
+        for j in range(2):
+            ffn_copy(step, j).start()
+    for step in range(2):
+        cols = span(step, 512)
         own[:, cols] = contract(act[span(x, ROWS), :], w_down[:, cols], 1, 0)
 
     def bump(row, value):
@@ -731,9 +741,9 @@
     local_cot.wait()
     cot_here = cotb.at[span(1 - y, CHUNK)]
     remote(cot.at[1 - y], cot_here, done.at[0], yr.at[Y_COT], at_y).wait_recv()
-    for step in range(4):
-        ffn_copy(step).wait()
     for j in range(2):
+        for step in range(4):
+            ffn_copy(step, j).wait()
         tiles(j, second_norm)
         x_rows(X_DA2, j, aw).start()
     out_here = pltpu.make_async_copy(outb.at[span(y, CHUNK)], out.at[y], os.at[0])
@@ -896,16 +906,17 @@
                     rz[r, k - 1] = jnp.zeros(rz.shape[2:], BF)
 
     def grad_down(i, carry):
-        half, yy = 1 - i // 2, i % 2
+        half, yy = i // 2, i % 2
         value = contract(act[:, span(yy * 2 + half, 512)], aw[...], 0, 0).astype(BF)
         for d in range(8):
             g_down[half, d % 2, yy, d // 2] = value[:, d * 128:(d + 1) * 128]
         return carry
 
     lax.fori_loop(0, 2, grad_down, 0)
+    core_send(U_DA)
+    lax.fori_loop(2, 4, grad_down, 0)
     core_send(U_DB)
-    lax.fori_loop(2, 4, grad_down, 0)
-    core_send(U_DA)
+    start(U_DA)
     start(U_DB)
 
     def grad_up(index, carry):
@@ -920,7 +931,7 @@
     lax.fori_loop(0, 4, grad_up, 0)
     core_send(U_UA)
     core_send(U_UB)
-    for u in (U_DA, U_UA, U_UB):
+    for u in (U_UA, U_UB):
         start(u)
 
     def back_norm(r, g):
@@ -947,7 +958,9 @@
         dctx[rows, :] = contract(a1w[rows, :], w_out[...], 1, 1).astype(BF)
         return carry
 
-    lax.fori_loop(0, 4, ctx_back, 0)
+    lax.fori_loop(0, 2, ctx_back, 0)
+    y_to_z(U_DB)
+    lax.fori_loop(2, 4, ctx_back, 0)
 
     def attend_back(pair, carry):
         lanes = span(pair, 128)
@@ -993,8 +1006,10 @@
 
     grad_out()
     core_send(U_OUT)
-    y_to_z(U_DB)
-    lax.fori_loop(0, 4, attend_back, 0)
+    lax.fori_loop(0, 2, attend_back, 0)
+    z_relay(U_DB, 0)
+    y_to_z(U_UA)
+    lax.fori_loop(2, 4, attend_back, 0)
 
     for row in range(2, 8):
         line = jnp.sum(acc[row], axis=0, keepdims=True)
@@ -1032,8 +1047,7 @@
 
     lax.fori_loop(0, 2, input_back, 0)
     start(U_OUT)
-    z_relay(U_DB, 0)
-    y_to_z(U_UA)
+    z_to_y(U_DA)
     vec_x.wait()
     vg[...] = vg[...] + vgx[...]
     vec_c.start()
@@ -1056,6 +1070,7 @@
     vec_y.start()
     for u in (U_Q, U_K, U_V):
         start(u)
+    z_relay(U_UA, 0)
     y_to_z(U_UB)
     lax.fori_loop(2, 4, input_back, 0)
     z_relay(U_OUT, 1)
@@ -1081,12 +1096,10 @@
     last_sum(y, False)
     gtok_here = pltpu.make_async_copy(da.at[span(y, CHUNK)], gtok.at[y], os.at[9])
     gtok_here.start()
-    z_relay(U_UA, 0)
+    z_relay(U_UB, 0)
     y_to_z(U_Q)
-    z_to_y(U_DA)
+    z_to_y(U_OUT)
     y_to_z(U_K)
-    z_relay(U_UB, 0)
-    z_to_y(U_OUT)
     y_to_z(U_V)
     for u in (U_Q, U_K, U_V):
         z_relay(u, 0)
@@ -1118,9 +1131,38 @@
         def _(copy=copy):
             copy.wait_send()
     for m in range(W_KINDS):
-        remote(half_of(m), half_of(m), wsc.at[m], wrc.at[m], at_c).wait_send()
+        remote(half_of(m), half_of(m), done.at[0], wrc.at[m], at_c).wait_send()
     for copy in finals + [out_here, gtok_here, gtok_there, vec_here]:
         copy.wait()
+
+
+def settle_kernel(*refs):
+    count = (len(refs) - 2) // 3
+    sources, dests, held = refs[:count], refs[count:2 * count], refs[2 * count:3 * count]
+    into, out_of = refs[3 * count:]
+    first = [pltpu.make_async_copy(s, h, into.at[i]) for i, (s, h) in enumerate(zip(sources, held))]
+    second = [pltpu.make_async_copy(h, d, out_of.at[i]) for i, (h, d) in enumerate(zip(held, dests))]
+    for copy in first:
+        copy.start()
+    for before, after in zip(first, second):
+        before.wait()
+        after.start()
+    for copy in second:
+        copy.wait()
+
+
+def settle(results):
+    shapes = [jax.ShapeDtypeStruct(r.shape, r.dtype) for r in results]
+    count = len(shapes)
+    hbm = pl.BlockSpec(memory_space=pl.ANY)
+    return pl.pallas_call(
+        settle_kernel,
+        out_shape=shapes,
+        in_specs=[hbm] * count,
+        out_specs=[hbm] * count,
+        scratch_shapes=[pltpu.VMEM(r.shape, r.dtype) for r in shapes]
+        + [pltpu.SemaphoreType.DMA((count,))] * 2,
+    )(*results)
 
 
 def layer(tokens, segment_ids, w_qkv, w_out, w_up, w_down, vectors, cotangent):
@@ -1163,13 +1205,13 @@
         vmem((2, 4, 16, 128), F32), vmem((2, 4, 16, 128), F32), vmem((4, 16, 128), F32),
         vmem((4, 16, 128), F32), vmem((3, 16, 128), F32), vmem((16, 128), F32),
         vmem((SEQ, 128), F32), vmem((SEQ, 128), F32),
-        dma((1,)), dma((8, 2, 3)), dma((8, 4)), dma((8,)), dma((8,)), dma((2, 4)), dma((4,)), dma((4,)),
+        dma((1,)), dma((8, 2, 3)), dma((8, 4)), dma((8,)), dma((2, 4)), dma((4, 2)), dma((4, 2)),
         dma((8, 2)), dma((8, 2)), dma((4,)),
         dma((8,)), dma((8,)), dma((8, 2, 4)),
         dma((6,)), dma((6,)), dma((10,)), dma((12,)),
     ]
     hbm = pl.BlockSpec(memory_space=pl.ANY)
-    return pl.pallas_call(
+    results = pl.pallas_call(
         layer_kernel,
         out_shape=outs,
         in_specs=[hbm, pl.BlockSpec(memory_space=pltpu.VMEM)] + [hbm] * 6,
@@ -1179,6 +1221,7 @@
             collective_id=0, has_side_effects=True, vmem_limit_bytes=67043328
         ),
     )(tokens, segment_ids, w_qkv, w_out, w_up, w_down, vectors, cotangent)
+    return settle(results)
 
 
 def solution(mesh):

time: 193 us -> 184 us (0.953)
  local copies, waits for them, and re-layouts: 7.47 us -> 0 us
  Pallas kernels: 185 us -> 183 us
    unnamed x19 -> x0, local copies, waits for them, and re-layouts: 7.47 us -> none
    pallas_call x1, Pallas kernels: 185 us -> 180 us  [layer(): pl.pallas_call(layer_kernel, out_shape=outs, in_specs=[hbm, pl.BlockSpec(...]
    pallas_call x0 -> x1, Pallas kernels: none -> 3 us  [settle(): pl.pallas_call(settle_kernel, out_shape=shapes, in_specs=[hbm] * count, o...]
where the time goes in v4:
time: 184 us
  Pallas kernels  183 us (99%)
    pallas_call x1, Pallas kernels, layer(): pl.pallas_call(layer_kernel, out_shape=outs, in_specs=[hbm, pl.BlockSpec(...  180 us

profile of v4, /device:TPU:0, one launch (start us, length us, event | category | flops | bytes accessed | tf_op | source)
XLA Modules:
  0.0 184.2 jit_solution(6463405623106442163)
XLA Ops:
  0.6 180.4 %shard_map.135 = (bf16[2,128,1024]{2,1,0:T(8,128)(2,1)}, f32[2,128,1024]{2,1,0:T(8,128)}, f32[3,128,256]{2,1,0:T(8,128)}, f32[256,128]{1,0:T(8,128)}, f32[128,10...) custom-call(bf16[2,128,1024]{2,1,0:T(8,128)(2,1)} %tok.1, s32[2,512]{1,0:T(2,128)} %seg.1, ...), custom_call_target="tpu_custom_call" | custom-call | tf_op jit(solution)/shard_map/pallas_call | solution.py:1214
  181.0 3.0 %shard_map.136 = (bf16[2,128,1024]{2,1,0:T(8,128)(2,1)}, f32[2,128,1024]{2,1,0:T(8,128)}, f32[3,128,256]{2,1,0:T(8,128)}, f32[256,128]{1,0:T(8,128)}, f32[128,10...) custom-call(bf16[2,128,1024]{2,1,0:T(8,128)(2,1)} %get-tuple-element.14.refs_0_, ...), custom_call_target="tpu_custom_call" | custom-call | tf_op jit(solution)/shard_map/pallas_call | solution.py:1158

commit v5 on v4

--- a/solution.py
+++ b/solution.py
@@ -271,7 +271,7 @@
 DIRECT = (W_VEC,)
 FAR_FIRST = ()
 U_DA, U_DB, U_UA, U_UB, U_OUT, U_V, U_K, U_Q = range(8)
-Z_FIRST = (U_DA, U_OUT)
+Z_FIRST = (U_DA,)
 R_BQ, R_BV, R_BO, R_G1, R_C1, R_BD, R_G2, R_C2, R_BU = range(9)
 ZS = 4
 SEQ = 512
@@ -559,31 +559,31 @@
     def two_blocks(ref, t, lanes):
         return jnp.concatenate([ref[span(t, 128), lanes], ref[span(t + 2, 128), lanes]], axis=0)
 
-    def attend(index, carry):
-        pair, t = index // 2, index % 2
+    def attend(pair, carry):
         lanes = span(pair, 128)
-        keys = pl.ds(pl.multiple_of(t * 128, 128), WINDOW)
-        query = two_blocks(qkv.at[0], t, lanes)
-        key, value = qkv[1, keys, lanes], qkv[2, keys, lanes]
-        total = jnp.zeros((ROWS, 128), F32)
-        for h, half in enumerate(halves):
-            scores = contract(jnp.where(half, query, none), key, 1, 1) + bias[t]
-            top = jnp.max(scores, axis=1, keepdims=True)
-            weight = jnp.exp(scores - top)
-            share_of = 1.0 / jnp.sum(weight, axis=1, keepdims=True)
-            weight = (weight * share_of).astype(BF)
-            prob[pair * 4 + t * 2 + h] = weight
-            total = total + contract(weight, jnp.where(half, value, none), 1, 0)
-        total = total.astype(BF)
-        ctx[span(t, 128), lanes] = total[:128]
-        ctx[span(t + 2, 128), lanes] = total[128:]
+        for t in range(2):
+            keys = pl.ds(t * 128, WINDOW)
+            query = two_blocks(qkv.at[0], t, lanes)
+            key, value = qkv[1, keys, lanes], qkv[2, keys, lanes]
+            total = jnp.zeros((ROWS, 128), F32)
+            for h, half in enumerate(halves):
+                scores = contract(jnp.where(half, query, none), key, 1, 1) + bias[t]
+                top = jnp.max(scores, axis=1, keepdims=True)
+                weight = jnp.exp(scores - top)
+                share_of = 1.0 / jnp.sum(weight, axis=1, keepdims=True)
+                weight = (weight * share_of).astype(BF)
+                prob[pair * 4 + t * 2 + h] = weight
+                total = total + contract(weight, jnp.where(half, value, none), 1, 0)
+            total = total.astype(BF)
+            ctx[t * 128:t * 128 + 128, lanes] = total[:128]
+            ctx[t * 128 + 256:t * 128 + 384, lanes] = total[128:]
         return carry
 
     z_serve(W_UP, 0, 0)
-    lax.fori_loop(0, 4, attend, 0)
+    lax.fori_loop(0, 2, attend, 0)
     for step in range(4):
         y_serve(W_OUT, step)
-    lax.fori_loop(4, 8, attend, 0)
+    lax.fori_loop(2, 4, attend, 0)
     up_early, up_late = z_serve_split(W_UP, 0, 1, middle, edge)
     up_early()
     z_send(W_DOWN, 0)
@@ -698,8 +698,6 @@
     y_serve(W_DOWN, 1)
     lax.fori_loop(3, 4, ffn_up, 0)
     y_serve(W_DOWN, 2)
-    z_serve(W_REST, 0, 2)
-    z_serve(W_REST, 1, 2)
     go_on(remote(cot.at[1 - y], cotb.at[span(y, CHUNK)], done.at[0], yr.at[Y_COT], at_y))
 
     def ffn_copy(step, j):
@@ -714,6 +712,9 @@
     for step in range(4):
         if step == 2:
             y_serve(W_DOWN, 3)
+        if step == 3:
+            z_serve(W_REST, 0, 2)
+            z_serve(W_REST, 1, 2)
         wait_down(step)
         cols = span(source_of(step), 256)
         stage[:, cols] = contract(act[span(1 - x, ROWS), :], w_down[:, cols], 1, 0).astype(BF)
@@ -1007,6 +1008,7 @@
     grad_out()
     core_send(U_OUT)
     lax.fori_loop(0, 2, attend_back, 0)
+    start(U_OUT)
     z_relay(U_DB, 0)
     y_to_z(U_UA)
     lax.fori_loop(2, 4, attend_back, 0)
@@ -1046,8 +1048,6 @@
         return carry
 
     lax.fori_loop(0, 2, input_back, 0)
-    start(U_OUT)
-    z_to_y(U_DA)
     vec_x.wait()
     vg[...] = vg[...] + vgx[...]
     vec_c.start()
@@ -1073,8 +1073,8 @@
     z_relay(U_UA, 0)
     y_to_z(U_UB)
     lax.fori_loop(2, 4, input_back, 0)
-    z_relay(U_OUT, 1)
-    z_relay(U_OUT, 0)
+    y_to_z(U_OUT)
+    z_to_y(U_DA)
     vec_y.wait()
     vg[c] = vg[c] + vgy[...]
     for k in range(1, ZS):
@@ -1098,7 +1098,7 @@
     gtok_here.start()
     z_relay(U_UB, 0)
     y_to_z(U_Q)
-    z_to_y(U_OUT)
+    z_relay(U_OUT, 0)
     y_to_z(U_K)
     y_to_z(U_V)
     for u in (U_Q, U_K, U_V):
@@ -1189,7 +1189,7 @@
     for y_shape, z_shape in (((4,), (1,)), ((1, 3), (2, 3)), ((1,), (2,))):
         scratch += [
             vmem(z_shape + half_down, BF), vmem(y_shape + half_down, BF),
-            vmem((2,) + y_shape + half_up, BF), vmem(z_shape + piece_out, BF),
+            vmem((2,) + y_shape + half_up, BF), vmem(y_shape + piece_out, BF),
             vmem((3,) + y_shape + piece_qkv, BF),
         ]
     scratch += [vmem((3, 128, 256), F32), vmem((256, 128), F32), vmem((128, 1024), F32), vmem((1024, 128), F32)]

time: 184 us -> 178 us (0.967)
  Pallas kernels: 183 us -> 176 us
    pallas_call x1, Pallas kernels: 180 us -> 173 us  [layer(): pl.pallas_call(layer_kernel, out_shape=outs, in_specs=[hbm, pl.BlockSpec(...]
where the time goes in v5:
time: 178 us; the launch traced here: 177 us
  Pallas kernels  176 us (99%)
    pallas_call x1, Pallas kernels, layer(): pl.pallas_call(layer_kernel, out_shape=outs, in_specs=[hbm, pl.BlockSpec(...  173 us

profile of v5, /device:TPU:0, one launch (start us, length us, event | category | flops | bytes accessed | tf_op | source)
XLA Modules:
  0.0 177.0 jit_solution(1327340892896840801)
XLA Ops:
  0.6 173.2 %shard_map.135 = (bf16[2,128,1024]{2,1,0:T(8,128)(2,1)}, f32[2,128,1024]{2,1,0:T(8,128)}, f32[3,128,256]{2,1,0:T(8,128)}, f32[256,128]{1,0:T(8,128)}, f32[128,10...) custom-call(bf16[2,128,1024]{2,1,0:T(8,128)(2,1)} %tok.1, s32[2,512]{1,0:T(2,128)} %seg.1, ...), custom_call_target="tpu_custom_call" | custom-call | tf_op jit(solution)/shard_map/pallas_call | solution.py:1214
  173.8 3.0 %shard_map.136 = (bf16[2,128,1024]{2,1,0:T(8,128)(2,1)}, f32[2,128,1024]{2,1,0:T(8,128)}, f32[3,128,256]{2,1,0:T(8,128)}, f32[256,128]{1,0:T(8,128)}, f32[128,10...) custom-call(bf16[2,128,1024]{2,1,0:T(8,128)(2,1)} %get-tuple-element.14.refs_0_, ...), custom_call_target="tpu_custom_call" | custom-call | tf_op jit(solution)/shard_map/pallas_call | solution.py:1158

commit v6 on v5

--- a/solution.py
+++ b/solution.py
@@ -264,7 +264,7 @@
 
 
 Y_TOK, Y_COT, Y_OUT, Y_GTOK = range(4)
-X_TOK, X_MIX, X_NORM, X_FFN, X_DA2, X_DH, X_DA1, X_DX = range(8)
+X_MIX, X_DH, X_DX, X_TOK, X_NORM, X_DA2, X_DA1 = range(7)
 W_Q, W_K, W_V, W_OUT, W_UP, W_DOWN, W_REST, W_VEC = range(8)
 W_KINDS = 8
 Y_FIRST = (W_REST,)
@@ -272,6 +272,7 @@
 FAR_FIRST = ()
 U_DA, U_DB, U_UA, U_UB, U_OUT, U_V, U_K, U_Q = range(8)
 Z_FIRST = (U_DA,)
+DA_ROWS = 640
 R_BQ, R_BV, R_BO, R_G1, R_C1, R_BD, R_G2, R_C2, R_BU = range(9)
 ZS = 4
 SEQ = 512
@@ -302,8 +303,8 @@
     tok, seg, wq, wo, wu, wd, vec, cot,
     out, gtok, gq, go, gu, gd, gv,
     w_qkv, w_out, w_up, w_down, w_vec, vf,
-    g_down, g_up, g_out, g_qkv,
-    c_down, c_up, c_out, c_qkv,
+    g_da, g_db, g_up, g_out, g_qkv,
+    c_da, c_db, c_up, c_out, c_qkv,
     y_da, y_db, y_up, y_out, y_qkv,
     z_da, z_db, z_up, z_out, z_qkv,
     h_da, h_db, h_up, h_out, h_qkv,
@@ -335,9 +336,12 @@
 
     sent = []
 
+    quiet = []
+
     def go_on(copy):
         copy.start()
-        sent.append(copy)
+        if not quiet:
+            sent.append(copy)
 
     args = [wq.at[0], wq.at[1], wq.at[2], wo, wu, wd.at[0:512], wd.at[512:1024], vec]
     edge = jnp.logical_or(z == 0, z == ZS - 1)
@@ -351,7 +355,8 @@
         @pl.when(condition)
         def _():
             copy.start()
-        later.append((condition, copy))
+        if not quiet:
+            later.append((condition, copy))
 
     def place(m, yy, d):
         if m <= W_V:
@@ -370,6 +375,9 @@
     def from_z(k):
         return lax.rem(z + ZS - k, ZS)
 
+    def z_slot(m, r):
+        return 24 if r else m * 3
+
     def column(r):
         return y if r == 0 else 1 - y
 
@@ -379,7 +387,7 @@
         for k, there in (steps[2:] + steps[:2] if m in FAR_FIRST else steps):
             there = None if m in DIRECT else there
             copy = remote(
-                source, place(m, column(r), dp), done.at[0], wrz.at[m, r, k - 1],
+                source, place(m, column(r), dp), done.at[0], wrz.at[z_slot(m, r) + k - 1],
                 z_device(lax.rem(z + k, ZS)),
             )
             if there is None:
@@ -411,7 +419,7 @@
         hand_on = None
         if step == 1 and m not in DIRECT:
             hand_on = remote(
-                here, here, done.at[0], wrz.at[m, r, slot], z_device(jnp.where(z == 1, 0, 3)),
+                here, here, done.at[0], wrz.at[z_slot(m, r) + slot], z_device(jnp.where(z == 1, 0, 3)),
             )
         over_y = None
         if r == 0 and m not in Y_FIRST and m != W_VEC:
@@ -423,7 +431,7 @@
 
     def z_take(m, r, step, keep=False):
         k, here, hand_on, over_y = z_parts(m, r, step)
-        remote(here, here, done.at[0], wrz.at[m, r, k - 1], at_x).wait_recv()
+        remote(here, here, done.at[0], wrz.at[z_slot(m, r) + k - 1], at_x).wait_recv()
         if hand_on is not None:
             @pl.when(middle)
             def _():
@@ -479,7 +487,7 @@
         remote(half_of(m), half_of(m), done.at[0], wrc.at[m], at_c).wait_recv()
 
     def x_copy(kind, j, src, dst):
-        return remote(src, dst, xs.at[kind, j], xr.at[kind, j], at_x)
+        return remote(src, dst, xs.at[kind, j] if kind <= X_DX else done.at[0], xr.at[kind, j], at_x)
 
     def tok_rows(xx, yy):
         return pl.ds(pl.multiple_of(xx * ROWS + yy * CHUNK, CHUNK), CHUNK)
@@ -704,7 +712,7 @@
         cols = span(source_of(step), 256)
         return remote(
             stage.at[span(j, CHUNK), cols], recv.at[span(j, CHUNK), cols],
-            fs.at[step, j], fr.at[step, j], at_x,
+            fs.at[0], fr.at[j], at_x,
         )
 
     for j in range(2):
@@ -730,23 +738,28 @@
     def second_norm(r, g):
         h1 = n1[r, :] * row_of(R_G1) + row_of(R_C1)
         normal, inverse = normed(h1 + own[r, :] + recv[r, :].astype(F32) + row_of(R_BD))
+        own[r, :] = normal
+        grad = norm_back(normal, inverse, cotb[r, :].astype(F32) * row_of(R_G2))
+        da[r, :] = grad
+        aw[g, :] = grad.astype(BF)
+
+    def second_rest(r, g):
+        normal, dy = own[r, :], cotb[r, :].astype(F32)
         outb[r, :] = (normal * row_of(R_G2) + row_of(R_C2)).astype(BF)
-        dy = cotb[r, :].astype(F32)
         bump(R_G2, dy * normal)
         bump(R_C2, dy)
-        grad = norm_back(normal, inverse, dy * row_of(R_G2))
-        bump(R_BD, grad)
-        da[r, :] = grad
-        aw[g, :] = grad.astype(BF)
+        bump(R_BD, da[r, :])
 
     local_cot.wait()
     cot_here = cotb.at[span(1 - y, CHUNK)]
     remote(cot.at[1 - y], cot_here, done.at[0], yr.at[Y_COT], at_y).wait_recv()
     for j in range(2):
-        for step in range(4):
-            ffn_copy(step, j).wait()
+        half = recv.at[span(j, CHUNK)]
+        remote(half, half, fs.at[0], fr.at[j], at_x).wait_recv()
         tiles(j, second_norm)
         x_rows(X_DA2, j, aw).start()
+    for j in range(2):
+        tiles(j, second_rest)
     out_here = pltpu.make_async_copy(outb.at[span(y, CHUNK)], out.at[y], os.at[0])
     out_here.start()
     go_on(remote(outb.at[span(1 - y, CHUNK)], out.at[y], done.at[0], yr.at[Y_OUT], at_y))
@@ -762,11 +775,12 @@
         hand_over(X_DH, None, s, contract(slope[rows, :], w_up[...], 1, 1))
         return carry
 
+    remote(stage, stage, fs.at[0], fr.at[0], at_x).wait_send()
     lax.fori_loop(0, 4, ffn_back, 0)
 
     units = {
-        U_DA: (g_down.at[0], c_down.at[0], y_da, z_da, h_da, o_down.at[0:512], gd.at[0:512]),
-        U_DB: (g_down.at[1], c_down.at[1], y_db, z_db, h_db, o_down.at[512:1024], gd.at[512:1024]),
+        U_DA: (g_da, c_da, y_da, z_da, h_da, o_down.at[0:DA_ROWS], gd.at[0:DA_ROWS]),
+        U_DB: (g_db, c_db, y_db, z_db, h_db, o_down.at[DA_ROWS:1024], gd.at[DA_ROWS:1024]),
         U_OUT: (g_out, c_out, y_out, z_out, h_out, o_out, go),
     }
     for u, i in ((U_UA, 0), (U_UB, 1)):
@@ -808,12 +822,12 @@
     def rs_z_copy(u, r, k):
         g, rz = units[u][0], units[u][3]
         to = lax.rem(z + k, ZS)
-        return remote(g.at[c, column(r), to], rz.at[r, k - 1], done.at[0], grz.at[u, r, k - 1], z_device(to))
+        return remote(g.at[c, column(r), to], rz.at[r, k - 1], done.at[0], grz.at[(32 if r else u * 4) + k - 1], z_device(to))
 
     def rs_hand_on(u, r):
         g, rh = units[u][0], units[u][4]
         far = jnp.where(z == 0, ZS - 1, 0)
-        return remote(g.at[c, column(r), far], rh.at[r], done.at[0], grz.at[u, r, 3], z_device(jnp.where(z == 0, 1, 2)))
+        return remote(g.at[c, column(r), far], rh.at[r], done.at[0], grz.at[(32 if r else u * 4) + 3], z_device(jnp.where(z == 0, 1, 2)))
 
     def z_hand_on(u, r):
         go_if(edge, rs_hand_on(u, r))
@@ -894,7 +908,7 @@
                 value = value + ry[0, rows, :].astype(F32)
             o[rows, :] = value
         piece_loop(g.shape[3], body)
-        copy = pltpu.make_async_copy(o, dest, os.at[1 + u])
+        copy = pltpu.make_async_copy(o, dest, os.at[0])
         copy.start()
         finals.append(copy)
 
@@ -906,49 +920,82 @@
                     rz = units[u][3]
                     rz[r, k - 1] = jnp.zeros(rz.shape[2:], BF)
 
-    def grad_down(i, carry):
-        half, yy = i // 2, i % 2
-        value = contract(act[:, span(yy * 2 + half, 512)], aw[...], 0, 0).astype(BF)
-        for d in range(8):
-            g_down[half, d % 2, yy, d // 2] = value[:, d * 128:(d + 1) * 128]
-        return carry
-
-    lax.fori_loop(0, 2, grad_down, 0)
-    core_send(U_DA)
-    lax.fori_loop(2, 4, grad_down, 0)
-    core_send(U_DB)
-    start(U_DA)
-    start(U_DB)
-
-    def grad_up(index, carry):
-        i, n = index // 2, index % 2
-        value = contract(hw[:, span(i, 512)], slope[:, span(n, 1024)], 0, 0).astype(BF)
-        for d in range(4):
-            for part in range(2):
-                r = d * 128 + part * 64
-                g_up[part, d % 2, n, i * 2 + d // 2] = value[r:r + 64, :]
-        return carry
-
-    lax.fori_loop(0, 4, grad_up, 0)
-    core_send(U_UA)
-    core_send(U_UB)
+    def grad_down(u):
+        g, first, count = (g_da, 0, DA_ROWS) if u == U_DA else (g_db, DA_ROWS, 1024 - DA_ROWS)
+
+        def step(yy, carry):
+            rows = pl.ds(pl.multiple_of(yy * 1024 + first, 128), count)
+            value = contract(act[:, rows], aw[...], 0, 0).astype(BF)
+            for d in range(8):
+                g[d % 2, yy, d // 2] = value[:, d * 128:(d + 1) * 128]
+            return carry
+
+        lax.fori_loop(0, 2, step, 0)
+        core_send(u)
+
+    def grad_up():
+        def step(index, carry):
+            i, n = index // 2, index % 2
+            value = contract(hw[:, span(i, 512)], slope[:, span(n, 1024)], 0, 0).astype(BF)
+            for d in range(4):
+                for part in range(2):
+                    r = d * 128 + part * 64
+                    g_up[part, d % 2, n, i * 2 + d // 2] = value[r:r + 64, :]
+            return carry
+
+        lax.fori_loop(0, 4, step, 0)
+        core_send(U_UA)
+        core_send(U_UB)
+
+    quiet.append(True)
+
+    @pl.when(c == 0)
+    def _():
+        grad_down(U_DB)
+        start(U_DB)
+        grad_down(U_DA)
+        start(U_DA)
+        grad_up()
+
+    @pl.when(c == 1)
+    def _():
+        grad_down(U_DB)
+        grad_down(U_DA)
+        grad_up()
+        start(U_DB)
+        start(U_DA)
+
+    quiet.clear()
+    for u in (U_DB, U_DA, U_UA, U_UB):
+        sent.append(core_copy(u))
+    sent.append(rs_y_copy(U_DB))
+    for r in (1, 0):
+        later.append((edge, rs_hand_on(U_DA, r)))
+        later.append((z != ZS - 1, rs_z_copy(U_DA, r, 1)))
+        later.append((z != 0, rs_z_copy(U_DA, r, 3)))
+        later.append((edge, rs_z_copy(U_DA, r, 2)))
     for u in (U_UA, U_UB):
         start(u)
 
     def back_norm(r, g):
         grad = da[r, :] + own[r, :] + recv[r, :].astype(F32)
-        normal = n1[r, :]
-        bump(R_G1, grad * normal)
-        bump(R_C1, grad)
-        grad = norm_back(normal, inv1[r, 0:1], grad * row_of(R_G1))
-        bump(R_BO, grad)
+        own[r, :] = grad
+        grad = norm_back(n1[r, :], inv1[r, 0:1], grad * row_of(R_G1))
         da[r, :] = grad
         a1w[g, :] = grad.astype(BF)
+
+    def back_rest(r, g):
+        grad = own[r, :]
+        bump(R_G1, grad * n1[r, :])
+        bump(R_C1, grad)
+        bump(R_BO, da[r, :])
 
     for j in range(2):
         x_sum(X_DH, j).wait_recv()
         tiles(j, back_norm)
         x_rows(X_DA1, j, a1w).start()
+    for j in range(2):
+        tiles(j, back_rest)
 
     z_relay(U_DA, 1)
     z_relay(U_DA, 0)
@@ -1009,7 +1056,6 @@
     core_send(U_OUT)
     lax.fori_loop(0, 2, attend_back, 0)
     start(U_OUT)
-    z_relay(U_DB, 0)
     y_to_z(U_UA)
     lax.fori_loop(2, 4, attend_back, 0)
 
@@ -1034,7 +1080,7 @@
 
     def vec_z(k):
         to = lax.rem(z + k, ZS)
-        return remote(vg.at[c, to], vgz.at[k - 1], vs.at[2 + k], vr.at[2 + k], z_device(to))
+        return remote(vg.at[c, to], vgz.at[k - 1], done.at[0], vr.at[2 + k], z_device(to))
 
     vec_x.start()
 
@@ -1065,6 +1111,7 @@
     for kind, u in ((0, U_Q), (1, U_K), (2, U_V)):
         lax.fori_loop(kind * 2, kind * 2 + 2, grad_qkv, 0)
         core_send(u)
+    z_relay(U_DB, 0)
     vec_c.wait()
     vg[c] = vg[c] + vgc[...]
     vec_y.start()
@@ -1078,7 +1125,7 @@
     vec_y.wait()
     vg[c] = vg[c] + vgy[...]
     for k in range(1, ZS):
-        vec_z(k).start()
+        go_on(vec_z(k))
 
     def last_sum(j, other):
         x_sum(X_DX, j).wait_recv()
@@ -1094,7 +1141,7 @@
     last_sum(1 - y, True)
     go_on(remote(gts, gtr, done.at[0], yr.at[Y_GTOK], at_y))
     last_sum(y, False)
-    gtok_here = pltpu.make_async_copy(da.at[span(y, CHUNK)], gtok.at[y], os.at[9])
+    gtok_here = pltpu.make_async_copy(da.at[span(y, CHUNK)], gtok.at[y], os.at[0])
     gtok_here.start()
     z_relay(U_UB, 0)
     y_to_z(U_Q)
@@ -1104,15 +1151,15 @@
     for u in (U_Q, U_K, U_V):
         z_relay(u, 0)
     for k in range(1, ZS):
-        vec_z(k).wait()
+        vec_z(k).wait_recv()
     gvb[...] = vg[c, z] + vgz[0] + vgz[1] + vgz[2]
-    vec_here = pltpu.make_async_copy(gvb.at[0:12], gv, os.at[10])
+    vec_here = pltpu.make_async_copy(gvb.at[0:12], gv, os.at[0])
     vec_here.start()
     for u in (U_DA, U_DB, U_UA, U_UB):
         finish(u)
     remote(gts, gtr, done.at[0], yr.at[Y_GTOK], at_y).wait_recv()
     gtf[...] = gtr[...].astype(F32)
-    gtok_there = pltpu.make_async_copy(gtf, gtok.at[1 - y], os.at[11])
+    gtok_there = pltpu.make_async_copy(gtf, gtok.at[1 - y], os.at[0])
     gtok_there.start()
     finish(U_OUT)
     finish(U_Q)
@@ -1180,15 +1227,16 @@
         vmem((3, D, COLS), BF), vmem((COLS, D), BF), vmem((D, HID), BF), vmem((HID, D), BF),
         vmem((8, 12, 128), BF), vmem((16, D), F32),
     ]
-    half_down, half_up, piece_out, piece_qkv = (512, 128), (64, 1024), (256, 128), (128, 256)
+    part_da, part_db = (DA_ROWS, 128), (1024 - DA_ROWS, 128)
+    half_up, piece_out, piece_qkv = (64, 1024), (256, 128), (128, 256)
     for shape in ((2, 2, 4), (2, 4)):
         scratch += [
-            vmem((2,) + shape + half_down, BF), vmem((2,) + shape + half_up, BF),
+            vmem(shape + part_da, BF), vmem(shape + part_db, BF), vmem((2,) + shape + half_up, BF),
             vmem(shape + piece_out, BF), vmem((3,) + shape + piece_qkv, BF),
         ]
     for y_shape, z_shape in (((4,), (1,)), ((1, 3), (2, 3)), ((1,), (2,))):
         scratch += [
-            vmem(z_shape + half_down, BF), vmem(y_shape + half_down, BF),
+            vmem(z_shape + part_da, BF), vmem(y_shape + part_db, BF),
             vmem((2,) + y_shape + half_up, BF), vmem(y_shape + piece_out, BF),
             vmem((3,) + y_shape + piece_qkv, BF),
         ]
@@ -1205,10 +1253,10 @@
         vmem((2, 4, 16, 128), F32), vmem((2, 4, 16, 128), F32), vmem((4, 16, 128), F32),
         vmem((4, 16, 128), F32), vmem((3, 16, 128), F32), vmem((16, 128), F32),
         vmem((SEQ, 128), F32), vmem((SEQ, 128), F32),
-        dma((1,)), dma((8, 2, 3)), dma((8, 4)), dma((8,)), dma((2, 4)), dma((4, 2)), dma((4, 2)),
-        dma((8, 2)), dma((8, 2)), dma((4,)),
-        dma((8,)), dma((8,)), dma((8, 2, 4)),
-        dma((6,)), dma((6,)), dma((10,)), dma((12,)),
+        dma((1,)), dma((27,)), dma((7, 4)), dma((8,)), dma((2, 4)), dma((1,)), dma((2,)),
+        dma((3, 2)), dma((7, 2)), dma((4,)),
+        dma((8,)), dma((8,)), dma((36,)),
+        dma((3,)), dma((6,)), dma((10,)), dma((1,)),
     ]
     hbm = pl.BlockSpec(memory_space=pl.ANY)
     results = pl.pallas_call(

time: 178 us -> 174 us (0.978)
  Pallas kernels: 176 us -> 173 us
    pallas_call x1, Pallas kernels: 173 us -> 170 us  [layer(): pl.pallas_call(layer_kernel, out_shape=outs, in_specs=[hbm, pl.BlockSpec(...]
where the time goes in v6:
time: 174 us; the launch traced here: 173 us
  Pallas kernels  173 us (99%)
    pallas_call x1, Pallas kernels, layer(): pl.pallas_call(layer_kernel, out_shape=outs, in_specs=[hbm, pl.BlockSpec(...  170 us

profile of v6, /device:TPU:0, one launch (start us, length us, event | category | flops | bytes accessed | tf_op | source)
XLA Modules:
  0.0 173.5 jit_solution(7915512185492864356)
XLA Ops:
  0.6 169.6 %shard_map.135 = (bf16[2,128,1024]{2,1,0:T(8,128)(2,1)}, f32[2,128,1024]{2,1,0:T(8,128)}, f32[3,128,256]{2,1,0:T(8,128)}, f32[256,128]{1,0:T(8,128)}, f32[128,10...) custom-call(bf16[2,128,1024]{2,1,0:T(8,128)(2,1)} %tok.1, s32[2,512]{1,0:T(2,128)} %seg.1, ...), custom_call_target="tpu_custom_call" | custom-call | tf_op jit(solution)/shard_map/pallas_call | solution.py:1262
  170.3 3.0 %shard_map.136 = (bf16[2,128,1024]{2,1,0:T(8,128)(2,1)}, f32[2,128,1024]{2,1,0:T(8,128)}, f32[3,128,256]{2,1,0:T(8,128)}, f32[256,128]{1,0:T(8,128)}, f32[128,10...) custom-call(bf16[2,128,1024]{2,1,0:T(8,128)(2,1)} %get-tuple-element.14.refs_0_, ...), custom_call_target="tpu_custom_call" | custom-call | tf_op jit(solution)/shard_map/pallas_call | solution.py:1205

commit v7 on v6

--- a/solution.py
+++ b/solution.py
@@ -974,8 +974,12 @@
         later.append((z != ZS - 1, rs_z_copy(U_DA, r, 1)))
         later.append((z != 0, rs_z_copy(U_DA, r, 3)))
         later.append((edge, rs_z_copy(U_DA, r, 2)))
-    for u in (U_UA, U_UB):
-        start(u)
+    quiet.append(True)
+
+    @pl.when(c == 0)
+    def _():
+        start(U_UA)
+        start(U_UB)
 
     def back_norm(r, g):
         grad = da[r, :] + own[r, :] + recv[r, :].astype(F32)
@@ -994,6 +998,15 @@
         x_sum(X_DH, j).wait_recv()
         tiles(j, back_norm)
         x_rows(X_DA1, j, a1w).start()
+
+    @pl.when(c == 1)
+    def _():
+        start(U_UA)
+        start(U_UB)
+
+    quiet.clear()
+    sent.append(rs_y_copy(U_UA))
+    sent.append(rs_y_copy(U_UB))
     for j in range(2):
         tiles(j, back_rest)
 
@@ -1143,10 +1156,10 @@
     last_sum(y, False)
     gtok_here = pltpu.make_async_copy(da.at[span(y, CHUNK)], gtok.at[y], os.at[0])
     gtok_here.start()
+    y_to_z(U_Q)
     z_relay(U_UB, 0)
-    y_to_z(U_Q)
+    y_to_z(U_K)
     z_relay(U_OUT, 0)
-    y_to_z(U_K)
     y_to_z(U_V)
     for u in (U_Q, U_K, U_V):
         z_relay(u, 0)

time: 174 us -> 174 us (level)
  no operation moved by 1% of the time
where the time goes in v7:
time: 174 us; the launch traced here: 173 us
  Pallas kernels  173 us (99%)
    pallas_call x1, Pallas kernels, layer(): pl.pallas_call(layer_kernel, out_shape=outs, in_specs=[hbm, pl.BlockSpec(...  170 us

profile of v7, /device:TPU:0, one launch (start us, length us, event | category | flops | bytes accessed | tf_op | source)
XLA Modules:
  0.0 173.4 jit_solution(11274172569289902918)
XLA Ops:
  0.6 169.5 %shard_map.135 = (bf16[2,128,1024]{2,1,0:T(8,128)(2,1)}, f32[2,128,1024]{2,1,0:T(8,128)}, f32[3,128,256]{2,1,0:T(8,128)}, f32[256,128]{1,0:T(8,128)}, f32[128,10...) custom-call(bf16[2,128,1024]{2,1,0:T(8,128)(2,1)} %tok.1, s32[2,512]{1,0:T(2,128)} %seg.1, ...), custom_call_target="tpu_custom_call" | custom-call | tf_op jit(solution)/shard_map/pallas_call | solution.py:1275
  170.2 3.0 %shard_map.136 = (bf16[2,128,1024]{2,1,0:T(8,128)(2,1)}, f32[2,128,1024]{2,1,0:T(8,128)}, f32[3,128,256]{2,1,0:T(8,128)}, f32[256,128]{1,0:T(8,128)}, f32[128,10...) custom-call(bf16[2,128,1024]{2,1,0:T(8,128)(2,1)} %get-tuple-element.14.refs_0_, ...), custom_call_target="tpu_custom_call" | custom-call | tf_op jit(solution)/shard_map/pallas_call | solution.py:1218

commit v8 on v7

--- a/solution.py
+++ b/solution.py
@@ -1,3 +1,5 @@
+import functools
+
 import jax
 import jax.numpy as jnp
 from jax import lax
@@ -764,9 +766,10 @@
     out_here.start()
     go_on(remote(outb.at[span(1 - y, CHUNK)], out.at[y], done.at[0], yr.at[Y_OUT], at_y))
 
-    def ffn_back(s, carry):
+    def ffn_back(s, carry, wait=True):
         rows = rows_of(s)
-        arrived(X_DA2, s, aw)
+        if wait:
+            arrived(X_DA2, s, aw)
         for n in range(2):
             cols = slice(n * 1024, (n + 1) * 1024)
             grad = contract(aw[rows, :], w_down[cols, :], 1, 1) * slope[rows, cols].astype(F32)
@@ -776,7 +779,12 @@
         return carry
 
     remote(stage, stage, fs.at[0], fr.at[0], at_x).wait_send()
-    lax.fori_loop(0, 4, ffn_back, 0)
+    lax.fori_loop(0, 3, ffn_back, 0)
+    last_rows = aw.at[rows_of(jnp.int32(3))]
+    x_copy(X_DA2, 1, last_rows, last_rows).wait_recv()
+
+    def last_back():
+        lax.fori_loop(3, 4, functools.partial(ffn_back, wait=False), 0)
 
     units = {
         U_DA: (g_da, c_da, y_da, z_da, h_da, o_down.at[0:DA_ROWS], gd.at[0:DA_ROWS]),
@@ -953,6 +961,7 @@
     def _():
         grad_down(U_DB)
         start(U_DB)
+        last_back()
         grad_down(U_DA)
         start(U_DA)
         grad_up()
@@ -960,6 +969,7 @@
     @pl.when(c == 1)
     def _():
         grad_down(U_DB)
+        last_back()
         grad_down(U_DA)
         grad_up()
         start(U_DB)

time: 174 us -> 174 us (level)
  no operation moved by 1% of the time
where the time goes in v8:
time: 174 us; the launch traced here: 173 us
  Pallas kernels  172 us (99%)
    pallas_call x1, Pallas kernels, layer(): pl.pallas_call(layer_kernel, out_shape=outs, in_specs=[hbm, pl.BlockSpec(...  169 us

profile of v8, /device:TPU:0, one launch (start us, length us, event | category | flops | bytes accessed | tf_op | source)
XLA Modules:
  0.0 173.3 jit_solution(13163266468695263087)
XLA Ops:
  0.6 169.5 %shard_map.135 = (bf16[2,128,1024]{2,1,0:T(8,128)(2,1)}, f32[2,128,1024]{2,1,0:T(8,128)}, f32[3,128,256]{2,1,0:T(8,128)}, f32[256,128]{1,0:T(8,128)}, f32[128,10...) custom-call(bf16[2,128,1024]{2,1,0:T(8,128)(2,1)} %tok.1, s32[2,512]{1,0:T(2,128)} %seg.1, ...), custom_call_target="tpu_custom_call" | custom-call | tf_op jit(solution)/shard_map/pallas_call | solution.py:1285
  170.1 3.0 %shard_map.136 = (bf16[2,128,1024]{2,1,0:T(8,128)(2,1)}, f32[2,128,1024]{2,1,0:T(8,128)}, f32[3,128,256]{2,1,0:T(8,128)}, f32[256,128]{1,0:T(8,128)}, f32[128,10...) custom-call(bf16[2,128,1024]{2,1,0:T(8,128)(2,1)} %get-tuple-element.14.refs_0_, ...), custom_call_target="tpu_custom_call" | custom-call | tf_op jit(solution)/shard_map/pallas_call | solution.py:1228
